TPU v7x, 1024 devices: a whole 4x8x16 slice. The times are simulated.
1024 devices in a mesh: gx: 8 (over z_hi, core), gy: 16 (over z_lo, x), gz: 8 (over y).
Axes of the slice: x: 4, y: 8, z: 16 (z_hi: 4, z_lo: 4; z = z_hi * 4 + z_lo), core: 2. Of those that a mesh axis runs over, the one named last changes fastest.
Arguments:
- particle_fields: float32 [20, 8388608], P(None, ('gx', 'gy', 'gz')), may hold values from -4 to 4
- step_length: float32 [8388608], P(('gx', 'gy', 'gz')), may hold values from 0.1 to 1
- live_mask: int32 [8388608], P(('gx', 'gy', 'gz')), may hold values 0 or 1
- dest_cell: int32 [8388608], P(('gx', 'gy', 'gz')), may hold values from 0 to 511
- block_counts: int32 [1024, 6], P(('gx', 'gy', 'gz')), may hold values from 0 to 12, as said below
- block_lists: int32 [1024, 48], P(('gx', 'gy', 'gz')), may hold values from 0 to 87, as said below
Outputs:
- tile_sums: float32 [20, 524288], P(None, ('gx', 'gy', 'gz'))
Inputs may be any that keep to these rules, and one draw needn't show every extreme that they name: `block_counts`: columns are directions in the order x lower, x upper, z lower, z upper, y lower, y upper; a count is at most its section's span (6, 6 or 12) and may be 0; at every section some domain receives full spans from both neighbours. `block_lists`: per domain, 6 entries toward the lower x neighbour, 6 toward the upper, then 2 * 6 for z and 24 for y in the same way; entries are block numbers of the domain's pool at that section. Entries below their direction's count are valid: valid entries of one domain over all sections are distinct, and each names an own block or an appended block that its sender filled. Other entries are arbitrary numbers within the pool.
All inputs are finite; a program needn't handle non-finite values. No bound on the sum of `live_mask` on one device may be relied on, other than what follows from the above.
Results may differ from a plain program's by a relative error of at most 0.0003.
Values sent between devices are 32-bit elements; how exact they have to be, the bound alone decides.
A program may use at most 32 MiB of HBM per device.

v0:
```python
import jax
import jax.numpy as jnp
from jax import lax
from jax.sharding import PartitionSpec as P

CELLS = 512
CAP_X = 6
CAP_Z = 6
CAP_Y = 12


def padded_2(array, sides, width):
    for axis, dim in sides:
        devices, length = (lax.axis_size(axis), array.shape[dim])
        up = [(i, (i + 1) % devices) for i in range(devices)]
        down = [(j, i) for i, j in up]
        last = lax.slice_in_dim(array, length - width, length, axis=dim)
        initial = lax.slice_in_dim(array, 0, width, axis=dim)
        before = lax.ppermute(last, axis, up)
        after = lax.ppermute(initial, axis, down)
        array = jnp.concatenate([before, array, after], axis=dim)
    return array


def pick_blocks(holding, chosen, toward_lower, toward_upper):
    extent = chosen.shape[0] // 2
    picked = jnp.take(holding, chosen, axis=1)
    position = jnp.arange(2 * extent) % extent
    wanted = jnp.where(jnp.arange(2 * extent) < extent, toward_lower, toward_upper)
    usable = (position < wanted).astype(jnp.float32)
    return picked * usable[None, :, None]


def arrived(padded, extent):
    margin = extent * 128
    lower_part = padded[:, :margin]
    upper_part = padded[:, padded.shape[1] - margin :]
    return jnp.concatenate([lower_part, upper_part], axis=1).reshape(
        padded.shape[0], 2 * extent, 128
    )


def group_width(block_total):
    for stride in (16, 8, 4, 2):
        if block_total % stride == 0:
            return stride
    return 1


def bin_blocks(holding, weights, tile_count):
    row_count, block_count, lane_count = holding.shape
    field_count = row_count - 2
    stride = group_width(block_count) * lane_count
    weighted = (holding[:field_count] * weights[None]).reshape(
        field_count, block_count * lane_count
    )
    cell_row = holding[row_count - 1].reshape(block_count * lane_count)
    tile_values = jnp.arange(tile_count, dtype=jnp.float32)

    def add_group(counter, running):
        offset = counter * stride
        portion = lax.dynamic_slice_in_dim(weighted, offset, stride, 1)
        cell_slice = lax.dynamic_slice_in_dim(cell_row, offset, stride, 0)
        one_hot = (cell_slice[:, None] == tile_values[None, :]).astype(jnp.float32)
        return running + jnp.dot(
            portion, one_hot, precision=lax.Precision.HIGHEST, preferred_element_type=jnp.float32
        )

    return lax.fori_loop(
        0,
        block_count * lane_count // stride,
        add_group,
        jnp.zeros((field_count, tile_count), jnp.float32),
    )


def per_device(particle_fields, step_length, live_mask, dest_cell, block_counts, block_lists):
    field_count = particle_fields.shape[0]
    row_count = field_count + 2
    advanced = particle_fields[0:3] + step_length[None, :] * particle_fields[3:6]
    carried = jnp.concatenate(
        [
            advanced,
            particle_fields[3:],
            live_mask.astype(jnp.float32)[None, :],
            dest_cell.astype(jnp.float32)[None, :],
        ],
        axis=0,
    )
    blocks_held = carried.reshape(row_count, -1, 128)
    number = block_counts[0]
    entries = block_lists[0]
    first_end = 2 * CAP_X
    second_end = first_end + 2 * CAP_Z
    outgoing = pick_blocks(blocks_held, entries[:first_end], number[0], number[1])
    padded = padded_2(outgoing.reshape(row_count, -1), (("gx", 1),), CAP_X * 128)
    blocks_held = jnp.concatenate([blocks_held, arrived(padded, CAP_X)], axis=1)
    outgoing = pick_blocks(blocks_held, entries[first_end:second_end], number[2], number[3])
    padded = padded_2(outgoing.reshape(row_count, -1), (("gz", 1),), CAP_Z * 128)
    blocks_held = jnp.concatenate([blocks_held, arrived(padded, CAP_Z)], axis=1)
    outgoing = pick_blocks(blocks_held, entries[second_end:], number[4], number[5])
    block_index = jnp.arange(blocks_held.shape[1])
    limits = []
    for section_index, extent in enumerate((CAP_X, CAP_Z, CAP_Y)):
        for side_index in range(2):
            limits.append(jnp.broadcast_to(number[2 * section_index + side_index], (extent,)))
    wanted = jnp.concatenate(limits)
    position = jnp.concatenate(
        [jnp.arange(extent) for extent in (CAP_X, CAP_X, CAP_Z, CAP_Z, CAP_Y, CAP_Y)]
    )
    listed = (entries[:, None] == block_index[None, :]) & (position < wanted)[:, None]
    keep_block = 1.0 - jnp.any(listed, axis=0).astype(jnp.float32)
    weights = blocks_held[field_count] * keep_block[:, None]
    padded = padded_2(outgoing.reshape(row_count, -1), (("gy", 1),), CAP_Y * 128)
    landed = arrived(padded, CAP_Y)
    tile_sums = bin_blocks(blocks_held, weights, CELLS) + bin_blocks(
        landed, landed[field_count], CELLS
    )
    return tile_sums


def solution(mesh):
    placed = (
        P(None, ("gx", "gy", "gz")),
        P(("gx", "gy", "gz")),
        P(("gx", "gy", "gz")),
        P(("gx", "gy", "gz")),
        P(("gx", "gy", "gz"), None),
        P(("gx", "gy", "gz"), None),
    )
    return jax.shard_map(
        per_device,
        mesh=mesh,
        in_specs=placed,
        out_specs=P(None, ("gx", "gy", "gz")),
        check_vma=False,
    )
```

profile of v0, /device:TPU:24, one launch (start us, length us, event | category | flops | bytes accessed | tf_op | source)
XLA Modules:
  0.0 72.7 jit_solution(16694480893711995281)
XLA Ops:
  0.0 0.8 %fusion.17 = (s32[12]{0:T(128)S(1)}, s32[12]{0:T(128)S(1)}) fusion(s32[1,48]{1,0:T(1,128)} %param.15), kind=kLoop, calls=%fused_computation.61 | loop fusion | flops 72 | bytes 192 | tf_op jit(solution)/shard_map/jit(_take)/jit(_where)/select_n | solution.py:27
  0.8 0.8 %compare_and_fusion.1 = (pred[12]{0:T(512)(128)(4,1)S(1)}, pred[12]{0:T(512)(128)(4,1)S(1)}) fusion(s32[1,48]{1,0:T(1,128)} %param.15), kind=kLoop, calls=%fused_computation.54 | loop fusion | flops 144 | bytes 120 | tf_op jit(solution)/shard_map/jit(_take)/and | solution.py:27
  1.6 1.5 %fusion.24 = (s32[1,1]{1,0:T(1,128)}, s32[1,1]{1,0:T(1,128)}, s32[1,1]{1,0:T(1,128)}, s32[1,1]{1,0:T(1,128)}, s32[1,1]{1,0:T(1,128)}, /*index=5*/s32[1,1]{1,0:T(1,128)}) fusion(s32[1,6]{1,0:T(1,128)} %param.14), kind=kLoop, calls=%fused_computation.69 | loop fusion | bytes 48 | tf_op jit(solution)/shard_map/slice | solution.py:106
  3.2 1.3 %compare_convert_fusion.2 = f32[12]{0:T(128)S(1)} fusion(s32[]{:T(128)} %bitcast.9, s32[]{:T(128)} %bitcast.8), kind=kLoop, calls=%fused_computation.55 | loop fusion | flops 120 | bytes 56 | tf_op jit(solution)/shard_map/convert_element_type | solution.py:30
  4.4 0.1 broadcast_bitcast_fusion.3
  4.5 1.2 %slice.104 = f32[17,8192]{1,0:T(8,128)S(1)} slice(f32[20,8192]{1,0:T(8,128)} %param.10), slice={[3:20], [0:8192]} | slice | bytes 1114112 | tf_op jit(solution)/shard_map/slice | solution.py:84
  5.7 0.1 copy.28
  5.9 0.3 copy.20
  6.3 0.3 copy-done.2
  6.6 1.1 %add_bitcast_fusion = f32[3,64,128]{2,0,1:T(4,128)S(1)} fusion(f32[20,8192]{1,0:T(8,128)} %param.10, f32[8192]{0:T(1024)S(1)} %copy-done.2), kind=kLoop, calls=%fused_computation.27 | loop fusion | flops 49152 | bytes 327680 | tf_op jit(solution)/shard_map/concatenate | solution.py:81
  7.7 0.2 pad_maximum_fusion.2
  7.9 0.6 gather_fusion
  8.6 0.1 broadcast_bitcast_fusion.4
  8.7 1.9 %collective-permute-start = (f32[22,768]{1,0:T(8,128)S(1)}, f32[22,768]{1,0:T(8,128)S(1)}, u32[]{:S(2)}, u32[]{:S(2)}) collective-permute-start(f32[22,768]{1,0:T(8,128)S(1)} %get-tuple-element.253), channel_id=1, source_target_pairs={{0,128},{128,256},{256,384},{384,512},{512,640},{640,768},{768,896... | collective-permute-start | bytes 202760 | tf_op jit(solution)/shard_map/ppermute | solution.py:19
  10.7 17.6 %collective-permute-start.1 = (f32[22,768]{1,0:T(8,128)S(1)}, f32[22,768]{1,0:T(8,128)S(1)}, u32[]{:S(2)}, u32[]{:S(2)}) collective-permute-start(f32[22,768]{1,0:T(8,128)S(1)} %get-tuple-element.254), channel_id=1, source_target_pairs={{128,0},{256,128},{384,256},{512,384},{640,512},{768,640},{896,768... | collective-permute-start | bytes 202760 | tf_op jit(solution)/shard_map/ppermute | solution.py:20
  28.3 0.1 fusion.18
  28.4 0.1 compare_and_fusion
  28.5 1.3 %compare_convert_fusion.1 = f32[12]{0:T(128)S(1)} fusion(s32[]{:T(128)} %bitcast.17, s32[]{:T(128)} %bitcast.16), kind=kLoop, calls=%fused_computation.53 | loop fusion | flops 120 | bytes 56 | tf_op jit(solution)/shard_map/convert_element_type | solution.py:30
  29.7 0.1 broadcast_bitcast_fusion.2
  29.8 1.3 %compare_convert_fusion = f32[24]{0:T(128)S(1)} fusion(s32[]{:T(128)} %bitcast.21, s32[]{:T(128)} %bitcast.20), kind=kLoop, calls=%fused_computation.49 | loop fusion | flops 240 | bytes 104 | tf_op jit(solution)/shard_map/convert_element_type | solution.py:30
  31.1 0.1 broadcast_bitcast_fusion
  31.1 0.1 broadcast_bitcast_fusion.1
  31.2 0.1 concatenate.51
  31.3 0.6 broadcast_in_dim.113
  31.9 0.6 broadcast_in_dim.114
  32.6 0.6 broadcast_in_dim.115
  33.1 0.7 broadcast_in_dim.116
  33.8 0.6 broadcast_in_dim.117
  34.5 0.6 broadcast_in_dim.118
  35.1 0.1 concatenate.52
  35.2 0.1 fusion.15
  35.5 0.2 pad_maximum_fusion.1
  35.7 0.6 gather_fusion.1
  36.4 4.7 %collective-permute-start.2 = (f32[22,768]{1,0:T(8,128)S(1)}, f32[22,768]{1,0:T(8,128)S(1)}, u32[]{:S(2)}, u32[]{:S(2)}) collective-permute-start(f32[22,768]{1,0:T(8,128)S(1)} %get-tuple-element.251), channel_id=1, source_target_pairs={{0,1},{1,2},{2,3},{3,4},{4,5},{5,6},{6,7},{7,0},{8,9},{9,10},{10,1... | collective-permute-start | bytes 202760 | tf_op jit(solution)/shard_map/ppermute | solution.py:19
  41.1 1.9 %collective-permute-start.3 = (f32[22,768]{1,0:T(8,128)S(1)}, f32[22,768]{1,0:T(8,128)S(1)}, u32[]{:S(2)}, u32[]{:S(2)}) collective-permute-start(f32[22,768]{1,0:T(8,128)S(1)} %get-tuple-element.252), channel_id=1, source_target_pairs={{1,0},{2,1},{3,2},{4,3},{5,4},{6,5},{7,6},{0,7},{9,8},{10,9},{11,1... | collective-permute-start | bytes 202760 | tf_op jit(solution)/shard_map/ppermute | solution.py:20
  43.1 5.5 %collective-permute-done.3 = f32[22,768]{1,0:T(8,128)S(1)} collective-permute-done((f32[22,768]{1,0:T(8,128)S(1)}, f32[22,768]{1,0:T(8,128)S(1)}, u32[]{:S(2)}, u32[]{:S(2)}) %collective-permute-start.3) | collective-permute-done | bytes 67616 | tf_op jit(solution)/shard_map/ppermute | solution.py:20
  48.7 0.2 pad_maximum_fusion
  48.8 0.6 gather_fusion.2
  49.4 0.1 copy.27
  49.5 0.1 copy.32
  49.7 3.4 %collective-permute-start.4 = (f32[22,1536]{1,0:T(8,128)S(1)}, f32[22,1536]{1,0:T(8,128)S(1)}, u32[]{:S(2)}, u32[]{:S(2)}) collective-permute-start(f32[22,1536]{1,0:T(8,128)S(1)} %get-tuple-element.250), channel_id=1, source_target_pairs={{0,8},{8,16},{16,24},{24,32},{32,40},{40,48},{48,56},{56,64},{64,7... | collective-permute-start | bytes 405512 | tf_op jit(solution)/shard_map/ppermute | solution.py:19
  53.1 6.4 %collective-permute-start.5 = (f32[22,1536]{1,0:T(8,128)S(1)}, f32[22,1536]{1,0:T(8,128)S(1)}, u32[]{:S(2)}, u32[]{:S(2)}) collective-permute-start(f32[22,1536]{1,0:T(8,128)S(1)} %get-tuple-element.249), channel_id=1, source_target_pairs={{8,0},{16,8},{24,16},{32,24},{40,32},{48,40},{56,48},{64,56},{72,6... | collective-permute-start | bytes 405512 | tf_op jit(solution)/shard_map/ppermute | solution.py:20
  59.4 0.2 fusion.19
  59.6 0.1 slice_multiply_fusion
  59.7 0.2 copy.26
  59.9 0.1 pad.24
  60.0 0.2 copy.31
  60.2 9.3 %while.28 = (s32[]{:T(128)}, f32[20,512]{1,0:T(8,128)S(1)}, f32[20,11264]{1,0:T(8,128)S(1)}, f32[11264]{0:T(1024)S(1)}, s32[]{:T(128)}, /*index=5*/s32[]{:T(128)}, s32[]{:T(128)}, s32[]{:T(128)}) while((s32[]{:T(128)}, f32[20,512]{1,0:T(8,128)S(1)}, f32[20,11264]{1,0:T(8,128)S(1)}, f32[11264]{0:T(1024)S(1)}, s32[]{:T(128)}, ...), condition=%wide.region_2.3_spmd.clone, body=%wide.region_1.2_spmd.clone.sunk | while | flops 126373896 | bytes 200853 | solution.py:69
  60.2 0.8 %fusion.30 = f32[20,512]{1,0:T(8,128)S(1)} fusion(f32[1024]{0:T(1024)S(1)} %dynamic_slice.41, f32[20,11264]{1,0:T(8,128)S(1)} %get-tuple-element.337, s32[]{:T(128)S(6)} %select_n.185, f32[20,512]{1,0:T(8,128)S(1)} %get-tuple-element.328, pred[]{:T(512)S(6)} %compare.6), kind=kOutput, calls=%fused_computation.7.clone.1 | convolution fusion | flops 126373888 | bytes 192517 | tf_op jit(solution)/shard_map/while/body/eval_jaxpr/dot_general | solution.py:65
  61.0 0.8 %fusion.30 = f32[20,512]{1,0:T(8,128)S(1)} fusion(f32[1024]{0:T(1024)S(1)} %dynamic_slice.41, f32[20,11264]{1,0:T(8,128)S(1)} %get-tuple-element.337, s32[]{:T(128)S(6)} %select_n.185, f32[20,512]{1,0:T(8,128)S(1)} %get-tuple-element.328, pred[]{:T(512)S(6)} %compare.6), kind=kOutput, calls=%fused_computation.7.clone.1 | convolution fusion | flops 126373888 | bytes 192517 | tf_op jit(solution)/shard_map/while/body/eval_jaxpr/dot_general | solution.py:65
  61.9 0.8 %fusion.30 = f32[20,512]{1,0:T(8,128)S(1)} fusion(f32[1024]{0:T(1024)S(1)} %dynamic_slice.41, f32[20,11264]{1,0:T(8,128)S(1)} %get-tuple-element.337, s32[]{:T(128)S(6)} %select_n.185, f32[20,512]{1,0:T(8,128)S(1)} %get-tuple-element.328, pred[]{:T(512)S(6)} %compare.6), kind=kOutput, calls=%fused_computation.7.clone.1 | convolution fusion | flops 126373888 | bytes 192517 | tf_op jit(solution)/shard_map/while/body/eval_jaxpr/dot_general | solution.py:65
  62.7 0.8 %fusion.30 = f32[20,512]{1,0:T(8,128)S(1)} fusion(f32[1024]{0:T(1024)S(1)} %dynamic_slice.41, f32[20,11264]{1,0:T(8,128)S(1)} %get-tuple-element.337, s32[]{:T(128)S(6)} %select_n.185, f32[20,512]{1,0:T(8,128)S(1)} %get-tuple-element.328, pred[]{:T(512)S(6)} %compare.6), kind=kOutput, calls=%fused_computation.7.clone.1 | convolution fusion | flops 126373888 | bytes 192517 | tf_op jit(solution)/shard_map/while/body/eval_jaxpr/dot_general | solution.py:65
  63.6 0.8 %fusion.30 = f32[20,512]{1,0:T(8,128)S(1)} fusion(f32[1024]{0:T(1024)S(1)} %dynamic_slice.41, f32[20,11264]{1,0:T(8,128)S(1)} %get-tuple-element.337, s32[]{:T(128)S(6)} %select_n.185, f32[20,512]{1,0:T(8,128)S(1)} %get-tuple-element.328, pred[]{:T(512)S(6)} %compare.6), kind=kOutput, calls=%fused_computation.7.clone.1 | convolution fusion | flops 126373888 | bytes 192517 | tf_op jit(solution)/shard_map/while/body/eval_jaxpr/dot_general | solution.py:65
  64.4 0.8 %fusion.30 = f32[20,512]{1,0:T(8,128)S(1)} fusion(f32[1024]{0:T(1024)S(1)} %dynamic_slice.41, f32[20,11264]{1,0:T(8,128)S(1)} %get-tuple-element.337, s32[]{:T(128)S(6)} %select_n.185, f32[20,512]{1,0:T(8,128)S(1)} %get-tuple-element.328, pred[]{:T(512)S(6)} %compare.6), kind=kOutput, calls=%fused_computation.7.clone.1 | convolution fusion | flops 126373888 | bytes 192517 | tf_op jit(solution)/shard_map/while/body/eval_jaxpr/dot_general | solution.py:65
  65.3 0.8 %fusion.30 = f32[20,512]{1,0:T(8,128)S(1)} fusion(f32[1024]{0:T(1024)S(1)} %dynamic_slice.41, f32[20,11264]{1,0:T(8,128)S(1)} %get-tuple-element.337, s32[]{:T(128)S(6)} %select_n.185, f32[20,512]{1,0:T(8,128)S(1)} %get-tuple-element.328, pred[]{:T(512)S(6)} %compare.6), kind=kOutput, calls=%fused_computation.7.clone.1 | convolution fusion | flops 126373888 | bytes 192517 | tf_op jit(solution)/shard_map/while/body/eval_jaxpr/dot_general | solution.py:65
  66.1 0.8 %fusion.30 = f32[20,512]{1,0:T(8,128)S(1)} fusion(f32[1024]{0:T(1024)S(1)} %dynamic_slice.41, f32[20,11264]{1,0:T(8,128)S(1)} %get-tuple-element.337, s32[]{:T(128)S(6)} %select_n.185, f32[20,512]{1,0:T(8,128)S(1)} %get-tuple-element.328, pred[]{:T(512)S(6)} %compare.6), kind=kOutput, calls=%fused_computation.7.clone.1 | convolution fusion | flops 126373888 | bytes 192517 | tf_op jit(solution)/shard_map/while/body/eval_jaxpr/dot_general | solution.py:65
  66.9 0.8 %fusion.30 = f32[20,512]{1,0:T(8,128)S(1)} fusion(f32[1024]{0:T(1024)S(1)} %dynamic_slice.41, f32[20,11264]{1,0:T(8,128)S(1)} %get-tuple-element.337, s32[]{:T(128)S(6)} %select_n.185, f32[20,512]{1,0:T(8,128)S(1)} %get-tuple-element.328, pred[]{:T(512)S(6)} %compare.6), kind=kOutput, calls=%fused_computation.7.clone.1 | convolution fusion | flops 126373888 | bytes 192517 | tf_op jit(solution)/shard_map/while/body/eval_jaxpr/dot_general | solution.py:65
  67.8 0.8 %fusion.30 = f32[20,512]{1,0:T(8,128)S(1)} fusion(f32[1024]{0:T(1024)S(1)} %dynamic_slice.41, f32[20,11264]{1,0:T(8,128)S(1)} %get-tuple-element.337, s32[]{:T(128)S(6)} %select_n.185, f32[20,512]{1,0:T(8,128)S(1)} %get-tuple-element.328, pred[]{:T(512)S(6)} %compare.6), kind=kOutput, calls=%fused_computation.7.clone.1 | convolution fusion | flops 126373888 | bytes 192517 | tf_op jit(solution)/shard_map/while/body/eval_jaxpr/dot_general | solution.py:65
  68.6 0.8 %fusion.30 = f32[20,512]{1,0:T(8,128)S(1)} fusion(f32[1024]{0:T(1024)S(1)} %dynamic_slice.41, f32[20,11264]{1,0:T(8,128)S(1)} %get-tuple-element.337, s32[]{:T(128)S(6)} %select_n.185, f32[20,512]{1,0:T(8,128)S(1)} %get-tuple-element.328, pred[]{:T(512)S(6)} %compare.6), kind=kOutput, calls=%fused_computation.7.clone.1 | convolution fusion | flops 126373888 | bytes 192517 | tf_op jit(solution)/shard_map/while/body/eval_jaxpr/dot_general | solution.py:65
  69.6 2.5 %while.29 = (s32[]{:T(128)}, f32[20,512]{1,0:T(8,128)S(1)}, f32[20,3072]{1,0:T(8,128)S(1)}, f32[3072]{0:T(1024)S(1)}, s32[]{:T(128)}, /*index=5*/s32[]{:T(128)}, s32[]{:T(128)}, s32[]{:T(128)}) while((s32[]{:T(128)}, f32[20,512]{1,0:T(8,128)S(1)}, f32[20,3072]{1,0:T(8,128)S(1)}, f32[3072]{0:T(1024)S(1)}, s32[]{:T(128)}, ...), condition=%wide.region_4.5_spmd.clone, body=%wide.region_3.4_spmd.clone.sunk | while | flops 126373896 | bytes 200853 | solution.py:69
  69.6 0.8 %fusion.32 = f32[20,512]{1,0:T(8,128)S(1)} fusion(f32[1024]{0:T(1024)S(1)} %dynamic_slice.43, f32[20,3072]{1,0:T(8,128)S(1)} %get-tuple-element.361, s32[]{:T(128)S(6)} %select_n.186, f32[20,512]{1,0:T(8,128)S(1)} %get-tuple-element.352, pred[]{:T(512)S(6)} %compare.7), kind=kOutput, calls=%fused_computation.13.clone.1 | convolution fusion | flops 126373888 | bytes 192517 | tf_op jit(solution)/shard_map/while/body/eval_jaxpr/dot_general | solution.py:65
  70.4 0.8 %fusion.32 = f32[20,512]{1,0:T(8,128)S(1)} fusion(f32[1024]{0:T(1024)S(1)} %dynamic_slice.43, f32[20,3072]{1,0:T(8,128)S(1)} %get-tuple-element.361, s32[]{:T(128)S(6)} %select_n.186, f32[20,512]{1,0:T(8,128)S(1)} %get-tuple-element.352, pred[]{:T(512)S(6)} %compare.7), kind=kOutput, calls=%fused_computation.13.clone.1 | convolution fusion | flops 126373888 | bytes 192517 | tf_op jit(solution)/shard_map/while/body/eval_jaxpr/dot_general | solution.py:65
  71.3 0.8 %fusion.32 = f32[20,512]{1,0:T(8,128)S(1)} fusion(f32[1024]{0:T(1024)S(1)} %dynamic_slice.43, f32[20,3072]{1,0:T(8,128)S(1)} %get-tuple-element.361, s32[]{:T(128)S(6)} %select_n.186, f32[20,512]{1,0:T(8,128)S(1)} %get-tuple-element.352, pred[]{:T(512)S(6)} %compare.7), kind=kOutput, calls=%fused_computation.13.clone.1 | convolution fusion | flops 126373888 | bytes 192517 | tf_op jit(solution)/shard_map/while/body/eval_jaxpr/dot_general | solution.py:65
  72.1 0.6 add.149
  (60 shorter events, 0.9 us)
Async XLA Ops:
  5.8 0.8 %copy-start.2 = (f32[8192]{0:T(1024)S(1)}, f32[8192]{0:T(1024)}, u32[]{:S(2)}) copy-start(f32[8192]{0:T(1024)} %param.11) | copy-start | bytes 98308
  5.9 1.8 %copy-start = (s32[8192]{0:T(1024)S(1)}, s32[8192]{0:T(1024)}, u32[]{:S(2)}) copy-start(s32[8192]{0:T(1024)} %param.12) | copy-start | bytes 98308
  5.9 1.8 %copy-start.1 = (s32[8192]{0:T(1024)S(1)}, s32[8192]{0:T(1024)}, u32[]{:S(2)}) copy-start(s32[8192]{0:T(1024)} %param.13) | copy-start | bytes 98308
  7.9 20.4 %copy-start.3 = (s32[1,48]{1,0:T(1,128)S(1)}, s32[1,48]{1,0:T(1,128)}, u32[]{:S(2)}) copy-start(s32[1,48]{1,0:T(1,128)} %param.15) | copy-start | bytes 580
  8.7 26.6 %collective-permute-start = (f32[22,768]{1,0:T(8,128)S(1)}, f32[22,768]{1,0:T(8,128)S(1)}, u32[]{:S(2)}, u32[]{:S(2)}) collective-permute-start(f32[22,768]{1,0:T(8,128)S(1)} %get-tuple-element.253), channel_id=1, source_target_pairs={{0,128},{128,256},{256,384},{384,512},{512,640},{640,768},{768,896... | collective-permute-start | bytes 202760 | tf_op jit(solution)/shard_map/ppermute | solution.py:19
  10.7 24.7 %collective-permute-start.1 = (f32[22,768]{1,0:T(8,128)S(1)}, f32[22,768]{1,0:T(8,128)S(1)}, u32[]{:S(2)}, u32[]{:S(2)}) collective-permute-start(f32[22,768]{1,0:T(8,128)S(1)} %get-tuple-element.254), channel_id=1, source_target_pairs={{128,0},{256,128},{384,256},{512,384},{640,512},{768,640},{896,768... | collective-permute-start | bytes 202760 | tf_op jit(solution)/shard_map/ppermute | solution.py:20
  36.4 6.7 %collective-permute-start.2 = (f32[22,768]{1,0:T(8,128)S(1)}, f32[22,768]{1,0:T(8,128)S(1)}, u32[]{:S(2)}, u32[]{:S(2)}) collective-permute-start(f32[22,768]{1,0:T(8,128)S(1)} %get-tuple-element.251), channel_id=1, source_target_pairs={{0,1},{1,2},{2,3},{3,4},{4,5},{5,6},{6,7},{7,0},{8,9},{9,10},{10,1... | collective-permute-start | bytes 202760 | tf_op jit(solution)/shard_map/ppermute | solution.py:19
  41.1 7.5 %collective-permute-start.3 = (f32[22,768]{1,0:T(8,128)S(1)}, f32[22,768]{1,0:T(8,128)S(1)}, u32[]{:S(2)}, u32[]{:S(2)}) collective-permute-start(f32[22,768]{1,0:T(8,128)S(1)} %get-tuple-element.252), channel_id=1, source_target_pairs={{1,0},{2,1},{3,2},{4,3},{5,4},{6,5},{7,6},{0,7},{9,8},{10,9},{11,1... | collective-permute-start | bytes 202760 | tf_op jit(solution)/shard_map/ppermute | solution.py:20
  49.7 19.8 %collective-permute-start.4 = (f32[22,1536]{1,0:T(8,128)S(1)}, f32[22,1536]{1,0:T(8,128)S(1)}, u32[]{:S(2)}, u32[]{:S(2)}) collective-permute-start(f32[22,1536]{1,0:T(8,128)S(1)} %get-tuple-element.250), channel_id=1, source_target_pairs={{0,8},{8,16},{16,24},{24,32},{32,40},{40,48},{48,56},{56,64},{64,7... | collective-permute-start | bytes 405512 | tf_op jit(solution)/shard_map/ppermute | solution.py:19
  53.1 16.4 %collective-permute-start.5 = (f32[22,1536]{1,0:T(8,128)S(1)}, f32[22,1536]{1,0:T(8,128)S(1)}, u32[]{:S(2)}, u32[]{:S(2)}) collective-permute-start(f32[22,1536]{1,0:T(8,128)S(1)} %get-tuple-element.249), channel_id=1, source_target_pairs={{8,0},{16,8},{24,16},{32,24},{40,32},{48,40},{56,48},{64,56},{72,6... | collective-permute-start | bytes 405512 | tf_op jit(solution)/shard_map/ppermute | solution.py:20
where the time goes:
time: 73.3 us; the launch traced here: 72.7 us
  starting transfers between devices  35.9 us (49%)
  matrix products  11.1 us (15%)
  local copies, waits for them, and re-layouts  10.7 us (15%)
  other arithmetic  8.33 us (11%)
  waiting for transfers between devices  5.53 us (8%)
    ppermute x3, starting transfers between devices, padded_2(): after = lax.ppermute(initial, axis, down)  25.9 us
    dot_general x14, matrix products, add_group(): jnp.dot(portion, one_hot, precision=lax.Precision.HIGHEST, preferred_elem...  11.1 us
    ppermute x3, starting transfers between devices, padded_2(): before = lax.ppermute(last, axis, up)  10 us
    ppermute x3, waiting for transfers between devices, padded_2(): after = lax.ppermute(initial, axis, down)  5.5 us
    convert_element_type x3, other arithmetic, pick_blocks(): usable = (position < wanted).astype(jnp.float32)  3.79 us
    broadcast_in_dim x6, local copies, waits for them, and re-layouts, per_device(): jnp.broadcast_to(number[2 * section_index + side_index], (extent,))  3.78 us
    gather x6, local copies, waits for them, and re-layouts, pick_blocks(): picked = jnp.take(holding, chosen, axis=1)  1.81 us
    slice x1, local copies, waits for them, and re-layouts, per_device(): number[2 * section_index + side_index]  1.54 us
  transfers between devices with their start and end apart: 6, of which 1 were waited for; matrix products, arithmetic and copies ran while one was open for 23% of the time, Pallas kernels for 0%

commit v1 on v0

v1 whole, which is shorter than its diff:
```python
import functools

import jax
import jax.numpy as jnp
from jax import lax
from jax.experimental import pallas as pl
from jax.experimental.pallas import tpu as pltpu
from jax.sharding import PartitionSpec as P

MESH = pl.DeviceIdType.MESH
FIELDS = 20
BLOCKS = 64
CELLS = 512
CAP_X = 6
CAP_Z = 6
CAP_Y = 12
LIST_LEN = 48
ROWS = 24
GROUP = 8
AXES = ("gx", "gy", "gz")


def kernel(
    sizes,
    fields_hbm,
    step_hbm,
    live_hbm,
    cell_hbm,
    counts_hbm,
    lists_hbm,
    out_ref,
    fields,
    step,
    live,
    cell,
    counts,
    lists,
    lists_vec,
    own,
    x_send,
    x_in,
    z_send,
    z_in,
    y_send,
    y_in,
    mask,
    acc,
    load_sem,
    send_sem,
    recv_sem,
):
    def beside(axis, shift):
        n = sizes[axis]
        return {axis: lax.rem(lax.axis_index(axis) + shift + n, n)}

    barrier = pltpu.get_barrier_semaphore()
    for axis in AXES:
        for shift in (-1, 1):
            pl.semaphore_signal(
                barrier, inc=1, device_id=beside(axis, shift), device_id_type=MESH
            )

    loads = [
        pltpu.make_async_copy(counts_hbm, counts, load_sem.at[0]),
        pltpu.make_async_copy(lists_hbm, lists, load_sem.at[1]),
        pltpu.make_async_copy(lists_hbm, lists_vec, load_sem.at[2]),
        pltpu.make_async_copy(step_hbm, step, load_sem.at[3]),
        pltpu.make_async_copy(live_hbm, live, load_sem.at[4]),
        pltpu.make_async_copy(cell_hbm, cell, load_sem.at[5]),
        pltpu.make_async_copy(fields_hbm, fields, load_sem.at[6]),
    ]
    for load in loads:
        load.start()
    for load in loads:
        load.wait()

    row = lax.broadcasted_iota(jnp.int32, (8, 128), 0)

    def prepare(block, _):
        columns = pl.ds(pl.multiple_of(block * 128, 128), 128)
        one = pl.ds(block, 1)
        weight = jnp.broadcast_to(live[one, :].astype(jnp.float32), (8, 128))
        length = jnp.broadcast_to(step[one, :], (8, 128))
        place = jnp.broadcast_to(cell[one, :].astype(jnp.float32), (8, 128))
        first = fields[0:8, columns]
        moved = first + length * pltpu.roll(first, 5, 0)
        first = jnp.where(row < 3, moved, first)
        tail = jnp.where(row[0:4] == 0, place[0:4], 0.0)
        last = jnp.concatenate([fields[16:20, columns] * weight[0:4], tail], axis=0)
        own[block, 0:8, :] = first * weight
        own[block, 8:16, :] = fields[8:16, columns] * weight
        own[block, 16:24, :] = last
        return 0

    lax.fori_loop(0, BLOCKS, prepare, 0, unroll=4)

    def pick(entry, usable, arrived):
        chosen = own[jnp.clip(entry, 0, BLOCKS - 1)]
        if arrived is not None:
            other = arrived[jnp.clip(entry - BLOCKS, 0, 2 * CAP_X - 1)]
            chosen = jnp.where(entry < BLOCKS, chosen, other)
        return jnp.where(usable, chosen, 0.0)

    def gather(first, count, extent, arrived, target):
        for slot in range(2 * extent):
            entry = lists[0, first + slot]
            usable = slot % extent < counts[0, count + slot // extent]
            target[slot] = pick(entry, usable, arrived)

    def exchange(axis, at, send, arrived, extent):
        copies = []
        for k, shift in ((0, 1), (1, -1)):
            source = pl.ds(extent, extent) if shift == 1 else pl.ds(0, extent)
            target = pl.ds(0, extent) if shift == 1 else pl.ds(extent, extent)
            copy = pltpu.make_async_remote_copy(
                src_ref=send.at[source],
                dst_ref=arrived.at[target],
                send_sem=send_sem.at[at + k],
                recv_sem=recv_sem.at[at + k],
                device_id=beside(axis, shift),
                device_id_type=MESH,
            )
            copy.start()
            copies.append(copy)
        return copies

    gather(0, 0, CAP_X, None, x_send)
    pl.semaphore_wait(barrier, 6)
    x_copies = exchange("gx", 0, x_send, x_in, CAP_X)

    lane = lax.broadcasted_iota(jnp.int32, (1, LIST_LEN), 1)
    limit = jnp.zeros((1, LIST_LEN), jnp.int32)
    begin = 0
    for column, extent in enumerate((CAP_X, CAP_X, CAP_Z, CAP_Z, CAP_Y, CAP_Y)):
        inside = (lane >= begin) & (lane < begin + extent)
        limit = jnp.where(inside, counts[0, column] + begin, limit)
        begin += extent
    named = jnp.where(lane < limit, lists_vec[...], -1)
    lower = (lane >= LIST_LEN - 2 * CAP_Y) & (lane < LIST_LEN - CAP_Y)
    upper = lane >= LIST_LEN - CAP_Y
    total = BLOCKS + 2 * CAP_X + 2 * CAP_Z
    block_id = lax.broadcasted_iota(jnp.int32, (total, LIST_LEN), 0)
    for k, part in enumerate((named, jnp.where(lower, named, -1), jnp.where(upper, named, -1))):
        found = jnp.where(block_id == part, 1.0, 0.0)
        found = jnp.max(found, axis=1, keepdims=True)
        if k == 0:
            found = 1.0 - found
        mask[k] = jnp.broadcast_to(found, (total, 128))

    tile = lax.broadcasted_iota(jnp.int32, (CELLS, 128), 0).astype(jnp.float32)

    def binned(source, start, at, blocks):
        hot, values = [], ([], [], [])
        for k in range(blocks):
            block = source[start + k]
            hot.append(jnp.where(tile == block[20:21, :], 1.0, 0.0).astype(jnp.bfloat16))
            high = block.astype(jnp.bfloat16).astype(jnp.float32)
            both = jnp.concatenate([high, block - high], axis=0)
            for c in range(3):
                weight = mask[c, pl.ds(at + k, 1), :]
                values[c].append((both * weight).astype(jnp.bfloat16))
        left = jnp.concatenate([jnp.concatenate(v, axis=1) for v in values], axis=0)
        right = jnp.concatenate(hot, axis=1)
        return lax.dot_general(
            left, right, (((1,), (1,)), ((), ())), preferred_element_type=jnp.float32
        )

    acc[...] = jnp.zeros_like(acc)

    def own_group(group, _):
        start = group * GROUP
        acc[...] += binned(own, start, start, GROUP)
        return 0

    lax.fori_loop(0, BLOCKS // GROUP, own_group, 0)

    for copy in x_copies:
        copy.wait_recv()
    gather(2 * CAP_X, 2, CAP_Z, x_in, z_send)
    z_copies = exchange("gz", 2, z_send, z_in, CAP_Z)
    acc[...] += binned(x_in, 0, BLOCKS, 2 * CAP_X)
    for copy in z_copies:
        copy.wait_recv()
    acc[...] += binned(z_in, 0, BLOCKS + 2 * CAP_X, 2 * CAP_Z)

    y_send[0] = acc[48:72] + acc[72:96]
    y_send[1] = acc[96:120] + acc[120:144]
    y_copies = exchange("gy", 4, y_send, y_in, 1)
    stay = acc[0:24] + acc[24:48]
    for copy in y_copies:
        copy.wait_recv()
    result = stay + y_in[0] + y_in[1]
    out_ref[...] = result[:FIELDS]
    for copy in x_copies + z_copies + y_copies:
        copy.wait_send()


def solution(mesh):
    sizes = dict(mesh.shape)

    def per_device(particle_fields, step_length, live_mask, dest_cell, block_counts, block_lists):
        anywhere = pl.BlockSpec(memory_space=pl.ANY)
        return pl.pallas_call(
            functools.partial(kernel, sizes),
            out_shape=jax.ShapeDtypeStruct((FIELDS, CELLS), jnp.float32),
            in_specs=[anywhere] * 6,
            out_specs=pl.BlockSpec(memory_space=pltpu.VMEM),
            scratch_shapes=[
                pltpu.VMEM((FIELDS, BLOCKS * 128), jnp.float32),
                pltpu.VMEM((BLOCKS, 128), jnp.float32),
                pltpu.VMEM((BLOCKS, 128), jnp.int32),
                pltpu.VMEM((BLOCKS, 128), jnp.int32),
                pltpu.SMEM((1, 6), jnp.int32),
                pltpu.SMEM((1, LIST_LEN), jnp.int32),
                pltpu.VMEM((1, LIST_LEN), jnp.int32),
                pltpu.VMEM((BLOCKS, ROWS, 128), jnp.float32),
                pltpu.VMEM((2 * CAP_X, ROWS, 128), jnp.float32),
                pltpu.VMEM((2 * CAP_X, ROWS, 128), jnp.float32),
                pltpu.VMEM((2 * CAP_Z, ROWS, 128), jnp.float32),
                pltpu.VMEM((2 * CAP_Z, ROWS, 128), jnp.float32),
                pltpu.VMEM((2, ROWS, CELLS), jnp.float32),
                pltpu.VMEM((2, ROWS, CELLS), jnp.float32),
                pltpu.VMEM((3, BLOCKS + 2 * CAP_X + 2 * CAP_Z, 128), jnp.float32),
                pltpu.VMEM((144, CELLS), jnp.float32),
                pltpu.SemaphoreType.DMA((7,)),
                pltpu.SemaphoreType.DMA((6,)),
                pltpu.SemaphoreType.DMA((6,)),
            ],
            compiler_params=pltpu.CompilerParams(collective_id=0, has_side_effects=True),
        )(
            particle_fields,
            step_length.reshape(BLOCKS, 128),
            live_mask.reshape(BLOCKS, 128),
            dest_cell.reshape(BLOCKS, 128),
            block_counts,
            block_lists,
        )

    placed = (P(None, AXES), P(AXES), P(AXES), P(AXES), P(AXES, None), P(AXES, None))
    return jax.shard_map(
        per_device, mesh=mesh, in_specs=placed, out_specs=P(None, AXES), check_vma=False
    )
```

time: 73.3 us -> 38.3 us (0.52)
  Pallas kernels: 0 us -> 36.7 us
  starting transfers between devices: 35.9 us -> 0 us
  matrix products: 11.1 us -> 0 us
  local copies, waits for them, and re-layouts: 10.7 us -> 1.42 us
  other arithmetic: 8.33 us -> 0 us
  waiting for transfers between devices: 5.53 us -> 0 us
    pallas_call x0 -> x1, Pallas kernels: none -> 36.7 us  [per_device(): pl.pallas_call(functools.partial(kernel, sizes), out_shape=jax.ShapeDtype...]
    ppermute x6 -> x0, starting transfers between devices: 35.9 us -> none  [the longest x3 25.9 us: padded_2(): after = lax.ppermute(initial, axis, down)]
    dot_general x14 -> x0, matrix products: 11.1 us -> none  [add_group(): jnp.dot(portion, one_hot, precision=lax.Precision.HIGHEST, preferred_elem...]
    ppermute x6 -> x0, waiting for transfers between devices: 5.53 us -> none  [the longest x3 5.5 us: padded_2(): after = lax.ppermute(initial, axis, down)]
    broadcast_in_dim x8 -> x0, local copies, waits for them, and re-layouts: 3.93 us -> none  [the longest x6 3.78 us: per_device(): jnp.broadcast_to(number[2 * section_index + side_index], (extent,))]
    convert_element_type x5 -> x0, other arithmetic: 3.8 us -> none  [the longest x3 3.79 us: pick_blocks(): usable = (position < wanted).astype(jnp.float32)]
    slice x6 -> x0, local copies, waits for them, and re-layouts: 2.8 us -> none  [the longest x1 1.54 us: per_device(): number[2 * section_index + side_index]]
    gather x6 -> x0, local copies, waits for them, and re-layouts: 1.81 us -> none  [pick_blocks(): picked = jnp.take(holding, chosen, axis=1)]
  transfers between devices with their start and end apart: 6 -> 0, of which waited for: 1 -> 0; matrix products, arithmetic and copies ran while one was open for 23% -> 0% of each run, Pallas kernels for 0% -> 0%
where the time goes in v1:
time: 38.3 us; the launch traced here: 38.1 us
  Pallas kernels  36.7 us (96%)
  local copies, waits for them, and re-layouts  1.42 us (4%)
    pallas_call x1, Pallas kernels, per_device(): pl.pallas_call(functools.partial(kernel, sizes), out_shape=jax.ShapeDtype...  36.7 us
    unnamed x1, local copies, waits for them, and re-layouts  1.42 us

profile of v1, /device:TPU:24, one launch (start us, length us, event | category | flops | bytes accessed | tf_op | source)
XLA Modules:
  0.0 38.1 jit_solution(394085595148180015)
XLA Ops:
  0.0 36.7 %shard_map.64 = f32[20,512]{1,0:T(8,128)} custom-call(f32[20,8192]{1,0:T(8,128)} %fields_hbm.1, f32[64,128]{1,0:T(8,128)} %bitcast.3, s32[64,128]{1,0:T(8,128)} %bitcast.4, s32[64,128]{1,0:T(8,128)} %bitcast.5, s32[1,6]{1,0:T(1,128)} %counts_hbm.1, s32[1,48]{1,0:T(1,128)} %lists_hbm.1), custom_call_target="tpu_custom_call" | custom-call | tf_op jit(solution)/shard_map/pallas_call | solution.py:203
  36.7 1.4 %copy.8 = f32[20,512]{1,0:T(8,128)} copy(f32[20,512]{1,0:T(8,128)} %shard_map.64) | data formatting | bytes 81920

commit v2 on v1

v2 whole, which is shorter than its diff:
```python
import functools

import jax
import jax.numpy as jnp
from jax import lax
from jax.experimental import pallas as pl
from jax.experimental.pallas import tpu as pltpu
from jax.sharding import PartitionSpec as P

MESH = pl.DeviceIdType.MESH
FIELDS = 20
BLOCKS = 64
CELLS = 512
CAP_X = 6
CAP_Z = 6
CAP_Y = 12
LIST_LEN = 48
ROWS = 24
GROUP = 8
AXES = ("gx", "gy", "gz")


def kernel(
    sizes,
    fields_hbm,
    step_hbm,
    live_hbm,
    cell_hbm,
    counts_hbm,
    lists_hbm,
    out_ref,
    fields,
    step,
    live,
    cell,
    counts,
    lists,
    lists_vec,
    own,
    x_send,
    far_in,
    near_in,
    z_send,
    z_in,
    z_far,
    note_send,
    note_in,
    y_send,
    y_in,
    mask,
    far_mask,
    acc,
    load_sem,
    send_sem,
    recv_sem,
):
    def beside(axis, shift):
        n = sizes[axis]
        return {axis: lax.rem(lax.axis_index(axis) + shift + n, n)}

    loads = [
        pltpu.make_async_copy(source, target, load_sem.at[k])
        for k, (source, target) in enumerate(
            (
                (lists_hbm, lists),
                (counts_hbm, counts),
                (lists_hbm, lists_vec),
                (step_hbm, step),
                (live_hbm, live),
                (cell_hbm, cell),
                (fields_hbm, fields),
            )
        )
    ]
    for load in loads:
        load.start()

    barrier = pltpu.get_barrier_semaphore()
    for axis in AXES:
        for shift in (-1, 1):
            pl.semaphore_signal(
                barrier, inc=1, device_id=beside(axis, shift), device_id_type=MESH
            )
    odd = lax.rem(lax.axis_index("gx"), 2)
    toward_far = 2 * odd - 1
    far_slot, near_slot = CAP_X * odd, CAP_X * (1 - odd)
    far_id, near_id = BLOCKS + far_slot, BLOCKS + near_slot

    for load in loads:
        load.wait()

    row = lax.broadcasted_iota(jnp.int32, (8, 128), 0)

    def carried(block):
        columns = pl.ds(pl.multiple_of(block * 128, 128), 128)
        one = pl.ds(block, 1)
        weight = jnp.broadcast_to(live[one, :].astype(jnp.float32), (8, 128))
        length = jnp.broadcast_to(step[one, :], (8, 128))
        place = jnp.broadcast_to(cell[one, :].astype(jnp.float32), (8, 128))
        first = fields[0:8, columns]
        moved = first + length * pltpu.roll(first, 5, 0)
        first = jnp.where(row < 3, moved, first)
        tail = jnp.where(row[0:4] == 0, place[0:4], 0.0)
        last = jnp.concatenate([fields[16:20, columns] * weight[0:4], tail], axis=0)
        return first * weight, fields[8:16, columns] * weight, last

    def prepare(block, _):
        for k, part in enumerate(carried(block)):
            own[block, 8 * k : 8 * k + 8, :] = part
        return 0

    lax.fori_loop(0, BLOCKS, prepare, 0, unroll=4)

    def usable(first, count, extent, slot):
        entry = lists[0, first + slot]
        return entry, slot % extent < counts[0, count + slot // extent]

    for slot in range(2 * CAP_X):
        entry, valid = usable(0, 0, CAP_X, slot)
        x_send[slot] = jnp.where(valid, own[jnp.clip(entry, 0, BLOCKS - 1)], 0.0)

    def remote(at, source, target, axis, shift):
        copy = pltpu.make_async_remote_copy(
            src_ref=source,
            dst_ref=target,
            send_sem=send_sem.at[at],
            recv_sem=recv_sem.at[at],
            device_id=beside(axis, shift),
            device_id_type=MESH,
        )
        copy.start()
        return copy

    pl.semaphore_wait(barrier, 6)
    far_copies = [
        remote(k, x_send.at[far_slot + k], far_in.at[k], "gx", toward_far)
        for k in range(CAP_X)
    ]
    near_copy = remote(6, x_send.at[pl.ds(near_slot, CAP_X)], near_in, "gx", -toward_far)

    lane = lax.broadcasted_iota(jnp.int32, (1, LIST_LEN), 1)
    limit = jnp.zeros((1, LIST_LEN), jnp.int32)
    begin = 0
    for column, extent in enumerate((CAP_X, CAP_X, CAP_Z, CAP_Z, CAP_Y, CAP_Y)):
        inside = (lane >= begin) & (lane < begin + extent)
        limit = jnp.where(inside, counts[0, column] + begin, limit)
        begin += extent
    named = jnp.where(lane < limit, lists_vec[...], -1)
    note_send[...] = jnp.full_like(note_send, -1.0)
    note_send[:, 0:LIST_LEN] = jnp.broadcast_to(named.astype(jnp.float32), (8, LIST_LEN))

    note_copies = [
        remote(7, note_send, note_in.at[0], "gz", 1),
        remote(8, note_send, note_in.at[1], "gz", -1),
    ]
    near_copy.wait_recv()
    for slot in range(2 * CAP_Z):
        entry, valid = usable(2 * CAP_X, 2, CAP_Z, slot)
        place = entry - near_id
        valid = valid & ((entry < BLOCKS) | ((place >= 0) & (place < CAP_X)))
        chosen = own[jnp.clip(entry, 0, BLOCKS - 1)]
        other = near_in[jnp.clip(place, 0, CAP_X - 1)]
        z_send[slot] = jnp.where(valid, jnp.where(entry < BLOCKS, chosen, other), 0.0)
    z_copies = [
        remote(9, z_send.at[pl.ds(CAP_Z, CAP_Z)], z_in.at[pl.ds(0, CAP_Z)], "gz", 1),
        remote(10, z_send.at[pl.ds(0, CAP_Z)], z_in.at[pl.ds(CAP_Z, CAP_Z)], "gz", -1),
    ]

    total = BLOCKS + 2 * CAP_X + 2 * CAP_Z
    first_y = LIST_LEN - 2 * CAP_Y
    block_id = lax.broadcasted_iota(jnp.int32, (total, LIST_LEN), 0)
    lower = (lane >= first_y) & (lane < first_y + CAP_Y)
    upper = lane >= first_y + CAP_Y
    for k, part in enumerate((named, jnp.where(lower, named, -1), jnp.where(upper, named, -1))):
        found = jnp.max(jnp.where(block_id == part, 1.0, 0.0), axis=1, keepdims=True)
        if k == 0:
            found = 1.0 - found
        mask[k] = jnp.broadcast_to(found, (total, 128))

    tile = lax.broadcasted_iota(jnp.int32, (CELLS, 128), 0).astype(jnp.float32)

    def binned(blocks):
        hot, values = [], ([], [], [])
        for block, weights in blocks:
            hot.append(jnp.where(tile == block[20:21, :], 1.0, 0.0).astype(jnp.bfloat16))
            high = block.astype(jnp.bfloat16).astype(jnp.float32)
            both = jnp.concatenate([high, block - high], axis=0)
            for c in range(3):
                values[c].append((both * weights[c]).astype(jnp.bfloat16))
        left = jnp.concatenate([jnp.concatenate(v, axis=1) for v in values], axis=0)
        right = jnp.concatenate(hot, axis=1)
        return lax.dot_general(
            left, right, (((1,), (1,)), ((), ())), preferred_element_type=jnp.float32
        )

    def weights_of(at):
        return [mask[c, pl.ds(at, 1), :] for c in range(3)]

    acc[...] = jnp.zeros_like(acc)

    def own_group(group, _):
        start = group * GROUP
        acc[...] += binned([(own[start + k], weights_of(start + k)) for k in range(GROUP)])
        return 0

    lax.fori_loop(0, BLOCKS // GROUP, own_group, 0)
    acc[...] += binned([(near_in[k], weights_of(near_id + k)) for k in range(CAP_X)])

    for copy in note_copies:
        copy.wait_recv()
    spot = lax.broadcasted_iota(jnp.int32, (1, 128), 1)
    first_z = 2 * CAP_X
    kept = spot - first_z
    kept = BLOCKS + 2 * CAP_X + jnp.where(kept < CAP_Z, kept + CAP_Z, kept - CAP_Z)
    at_row = lax.broadcasted_iota(jnp.int32, (LIST_LEN, 128), 0)
    at_lane = lax.broadcasted_iota(jnp.int32, (LIST_LEN, 128), 1)
    tall = jnp.broadcast_to(note_send[0:1, :], (LIST_LEN, 128))
    tall = jnp.sum(jnp.where(at_row == at_lane, tall, 0.0), axis=1, keepdims=True)
    same = jnp.where(tall == kept.astype(jnp.float32), 1.0, 0.0)
    down = jnp.max(same[first_y : first_y + CAP_Y], axis=0, keepdims=True)
    up = jnp.max(same[first_y + CAP_Y :], axis=0, keepdims=True)
    stay = 1.0 - down - up
    for side in range(2):
        begin = first_z + CAP_Z * (1 - side)
        inside = (spot >= begin) & (spot < begin + CAP_Z)
        sent = note_in[side] == (row + far_id).astype(jnp.float32)
        for c, kind in enumerate((stay, down, up)):
            hit = jnp.where(sent & inside, kind, 0.0)
            hit = jnp.max(hit, axis=1, keepdims=True)
            far_mask[side, c] = jnp.broadcast_to(hit, (8, 128))

    relays = []
    for k, copy in enumerate(far_copies):
        copy.wait_recv()
        relays.append(
            (
                remote(11 + 2 * k, far_in.at[k], z_far.at[0, k], "gz", 1),
                remote(12 + 2 * k, far_in.at[k], z_far.at[1, k], "gz", -1),
            )
        )
    acc[...] += binned([(far_in[k], weights_of(far_id + k)) for k in range(CAP_X)])
    for copy in z_copies:
        copy.wait_recv()
    z_id = BLOCKS + 2 * CAP_X
    acc[...] += binned([(z_in[k], weights_of(z_id + k)) for k in range(2 * CAP_Z)])
    for k, pair in enumerate(relays):
        for copy in pair:
            copy.wait_recv()
        acc[...] += binned(
            [
                (z_far[side, k], [far_mask[side, c, k : k + 1, :] for c in range(3)])
                for side in range(2)
            ]
        )

    y_send[0] = acc[48:72] + acc[72:96]
    y_send[1] = acc[96:120] + acc[120:144]
    y_copies = [
        remote(23, y_send.at[1], y_in.at[0], "gy", 1),
        remote(24, y_send.at[0], y_in.at[1], "gy", -1),
    ]
    result = acc[0:24] + acc[24:48]
    for copy in y_copies:
        copy.wait_recv()
    result = result + y_in[0] + y_in[1]
    out_ref[...] = result[:FIELDS]
    sent = far_copies + [near_copy] + note_copies + z_copies + y_copies
    for copy in sent + [copy for pair in relays for copy in pair]:
        copy.wait_send()


def solution(mesh):
    sizes = dict(mesh.shape)

    def per_device(particle_fields, step_length, live_mask, dest_cell, block_counts, block_lists):
        anywhere = pl.BlockSpec(memory_space=pl.ANY)
        return pl.pallas_call(
            functools.partial(kernel, sizes),
            out_shape=pltpu.VMEM((FIELDS, CELLS), jnp.float32),
            in_specs=[anywhere] * 6,
            out_specs=pl.BlockSpec(memory_space=pltpu.VMEM),
            scratch_shapes=[
                pltpu.VMEM((FIELDS, BLOCKS * 128), jnp.float32),
                pltpu.VMEM((BLOCKS, 128), jnp.float32),
                pltpu.VMEM((BLOCKS, 128), jnp.int32),
                pltpu.VMEM((BLOCKS, 128), jnp.int32),
                pltpu.SMEM((1, 6), jnp.int32),
                pltpu.SMEM((1, LIST_LEN), jnp.int32),
                pltpu.VMEM((1, LIST_LEN), jnp.int32),
                pltpu.VMEM((BLOCKS, ROWS, 128), jnp.float32),
                pltpu.VMEM((2 * CAP_X, ROWS, 128), jnp.float32),
                pltpu.VMEM((CAP_X, ROWS, 128), jnp.float32),
                pltpu.VMEM((CAP_X, ROWS, 128), jnp.float32),
                pltpu.VMEM((2 * CAP_Z, ROWS, 128), jnp.float32),
                pltpu.VMEM((2 * CAP_Z, ROWS, 128), jnp.float32),
                pltpu.VMEM((2, CAP_X, ROWS, 128), jnp.float32),
                pltpu.VMEM((8, 128), jnp.float32),
                pltpu.VMEM((2, 8, 128), jnp.float32),
                pltpu.VMEM((2, ROWS, CELLS), jnp.float32),
                pltpu.VMEM((2, ROWS, CELLS), jnp.float32),
                pltpu.VMEM((3, BLOCKS + 2 * CAP_X + 2 * CAP_Z, 128), jnp.float32),
                pltpu.VMEM((2, 3, 8, 128), jnp.float32),
                pltpu.VMEM((144, CELLS), jnp.float32),
                pltpu.SemaphoreType.DMA((7,)),
                pltpu.SemaphoreType.DMA((25,)),
                pltpu.SemaphoreType.DMA((25,)),
            ],
            compiler_params=pltpu.CompilerParams(collective_id=0, has_side_effects=True),
        )(
            particle_fields,
            step_length.reshape(BLOCKS, 128),
            live_mask.reshape(BLOCKS, 128),
            dest_cell.reshape(BLOCKS, 128),
            block_counts,
            block_lists,
        )

    placed = (P(None, AXES), P(AXES), P(AXES), P(AXES), P(AXES, None), P(AXES, None))
    return jax.shard_map(
        per_device, mesh=mesh, in_specs=placed, out_specs=P(None, AXES), check_vma=False
    )
```

time: 38.3 us -> 37.4 us (0.977)
  the two profiles are of different devices: /device:TPU:24 before, /device:TPU:1 now
where the time goes in v2:
time: 37.4 us; the launch traced here: 37.2 us
  Pallas kernels  36.6 us (98%)
  local copies, waits for them, and re-layouts  0.62 us (2%)
    pallas_call x1, Pallas kernels, per_device(): pl.pallas_call(functools.partial(kernel, sizes), out_shape=pltpu.VMEM((FI...  36.6 us

profile of v2, /device:TPU:1, one launch (start us, length us, event | category | flops | bytes accessed | tf_op | source)
XLA Modules:
  0.0 37.2 jit_solution(4219239929436221947)
XLA Ops:
  0.0 36.6 %shard_map.64 = f32[20,512]{1,0:T(8,128)S(1)} custom-call(f32[20,8192]{1,0:T(8,128)} %fields_hbm.1, f32[64,128]{1,0:T(8,128)} %bitcast.3, s32[64,128]{1,0:T(8,128)} %bitcast.4, s32[64,128]{1,0:T(8,128)} %bitcast.5, s32[1,6]{1,0:T(1,128)} %counts_hbm.1, s32[1,48]{1,0:T(1,128)} %lists_hbm.1), custom_call_target="tpu_custom_call" | custom-call | tf_op jit(solution)/shard_map/pallas_call | solution.py:277
  36.6 0.6 %copy.8 = f32[20,512]{1,0:T(8,128)} copy(f32[20,512]{1,0:T(8,128)S(1)} %shard_map.64) | data formatting | bytes 81920

commit v3 on v2

--- a/solution.py
+++ b/solution.py
@@ -17,6 +17,7 @@
 LIST_LEN = 48
 ROWS = 24
 GROUP = 8
+PARTS = ((0, 2), (2, 2), (4, 2))
 AXES = ("gx", "gy", "gz")
 
 
@@ -53,6 +54,7 @@
     load_sem,
     send_sem,
     recv_sem,
+    ready,
 ):
     def beside(axis, shift):
         n = sizes[axis]
@@ -75,14 +77,22 @@
     for load in loads:
         load.start()
 
+    gx = lax.axis_index("gx")
+    odd = lax.rem(gx, 2)
+    toward_far = 2 * odd - 1
+    early = (gx == 0) | ((odd == 1) & (gx != sizes["gx"] - 1))
     barrier = pltpu.get_barrier_semaphore()
-    for axis in AXES:
-        for shift in (-1, 1):
-            pl.semaphore_signal(
-                barrier, inc=1, device_id=beside(axis, shift), device_id_type=MESH
-            )
-    odd = lax.rem(lax.axis_index("gx"), 2)
-    toward_far = 2 * odd - 1
+
+    def greet(axis, shift):
+        pl.semaphore_signal(barrier, inc=1, device_id=beside(axis, shift), device_id_type=MESH)
+
+    for axis, shift in (("gz", -1), ("gz", 1), ("gy", -1), ("gy", 1), ("gx", -toward_far)):
+        greet(axis, shift)
+
+    @pl.when(early)
+    def _():
+        greet("gx", toward_far)
+
     far_slot, near_slot = CAP_X * odd, CAP_X * (1 - odd)
     far_id, near_id = BLOCKS + far_slot, BLOCKS + near_slot
 
@@ -119,8 +129,8 @@
         entry, valid = usable(0, 0, CAP_X, slot)
         x_send[slot] = jnp.where(valid, own[jnp.clip(entry, 0, BLOCKS - 1)], 0.0)
 
-    def remote(at, source, target, axis, shift):
-        copy = pltpu.make_async_remote_copy(
+    def describe(at, source, target, axis, shift):
+        return pltpu.make_async_remote_copy(
             src_ref=source,
             dst_ref=target,
             send_sem=send_sem.at[at],
@@ -128,14 +138,26 @@
             device_id=beside(axis, shift),
             device_id_type=MESH,
         )
+
+    def remote(*where):
+        copy = describe(*where)
         copy.start()
         return copy
 
-    pl.semaphore_wait(barrier, 6)
-    far_copies = [
-        remote(k, x_send.at[far_slot + k], far_in.at[k], "gx", toward_far)
-        for k in range(CAP_X)
-    ]
+    pl.semaphore_wait(barrier, jnp.where(early, 5, 6))
+    far_copies = []
+    for k, (at, size) in enumerate(PARTS):
+        source = x_send.at[pl.ds(far_slot + at, size)]
+        far_copies.append(describe(k, source, far_in.at[pl.ds(at, size)], "gx", toward_far))
+
+    @pl.when(jnp.logical_not(early))
+    def _():
+        pl.semaphore_signal(
+            ready, inc=1, device_id=beside("gx", toward_far), device_id_type=MESH
+        )
+        for copy in far_copies:
+            copy.start()
+
     near_copy = remote(6, x_send.at[pl.ds(near_slot, CAP_X)], near_in, "gx", -toward_far)
 
     lane = lax.broadcasted_iota(jnp.int32, (1, LIST_LEN), 1)
@@ -229,26 +251,35 @@
             hit = jnp.max(hit, axis=1, keepdims=True)
             far_mask[side, c] = jnp.broadcast_to(hit, (8, 128))
 
-    relays = []
-    for k, copy in enumerate(far_copies):
-        copy.wait_recv()
-        relays.append(
-            (
-                remote(11 + 2 * k, far_in.at[k], z_far.at[0, k], "gz", 1),
-                remote(12 + 2 * k, far_in.at[k], z_far.at[1, k], "gz", -1),
-            )
-        )
-    acc[...] += binned([(far_in[k], weights_of(far_id + k)) for k in range(CAP_X)])
     for copy in z_copies:
         copy.wait_recv()
     z_id = BLOCKS + 2 * CAP_X
     acc[...] += binned([(z_in[k], weights_of(z_id + k)) for k in range(2 * CAP_Z)])
-    for k, pair in enumerate(relays):
+
+    @pl.when(early)
+    def _():
+        pl.semaphore_wait(ready, 1)
+        for copy in far_copies:
+            copy.start()
+
+    relays = []
+    for k, copy in enumerate(far_copies):
+        copy.wait_recv()
+        part = pl.ds(*PARTS[k])
+        relays.append(
+            (
+                remote(11 + 2 * k, far_in.at[part], z_far.at[0, part], "gz", 1),
+                remote(12 + 2 * k, far_in.at[part], z_far.at[1, part], "gz", -1),
+            )
+        )
+    acc[...] += binned([(far_in[k], weights_of(far_id + k)) for k in range(CAP_X)])
+    for (at, size), pair in zip(PARTS, relays, strict=True):
         for copy in pair:
             copy.wait_recv()
         acc[...] += binned(
             [
                 (z_far[side, k], [far_mask[side, c, k : k + 1, :] for c in range(3)])
+                for k in range(at, at + size)
                 for side in range(2)
             ]
         )
@@ -304,6 +335,7 @@
                 pltpu.SemaphoreType.DMA((7,)),
                 pltpu.SemaphoreType.DMA((25,)),
                 pltpu.SemaphoreType.DMA((25,)),
+                pltpu.SemaphoreType.REGULAR,
             ],
             compiler_params=pltpu.CompilerParams(collective_id=0, has_side_effects=True),
         )(

time: 37.4 us -> 36.1 us (0.965)
  the two profiles are of different devices: /device:TPU:1 before, /device:TPU:24 now
where the time goes in v3:
time: 36.1 us; the launch traced here: 36 us
  Pallas kernels  35.3 us (98%)
  local copies, waits for them, and re-layouts  0.62 us (2%)
    pallas_call x1, Pallas kernels, per_device(): pl.pallas_call(functools.partial(kernel, sizes), out_shape=pltpu.VMEM((FI...  35.3 us

profile of v3, /device:TPU:24, one launch (start us, length us, event | category | flops | bytes accessed | tf_op | source)
XLA Modules:
  0.0 36.0 jit_solution(9912682635649434035)
XLA Ops:
  0.0 35.3 %shard_map.64 = f32[20,512]{1,0:T(8,128)S(1)} custom-call(f32[20,8192]{1,0:T(8,128)} %fields_hbm.1, f32[64,128]{1,0:T(8,128)} %bitcast.3, s32[64,128]{1,0:T(8,128)} %bitcast.4, s32[64,128]{1,0:T(8,128)} %bitcast.5, s32[1,6]{1,0:T(1,128)} %counts_hbm.1, s32[1,48]{1,0:T(1,128)} %lists_hbm.1), custom_call_target="tpu_custom_call" | custom-call | tf_op jit(solution)/shard_map/pallas_call | solution.py:308
  35.3 0.6 %copy.8 = f32[20,512]{1,0:T(8,128)} copy(f32[20,512]{1,0:T(8,128)S(1)} %shard_map.64) | data formatting | bytes 81920

commit v4 on v3

v4 whole, which is shorter than its diff:
```python
import functools

import jax
import jax.numpy as jnp
from jax import lax
from jax.experimental import pallas as pl
from jax.experimental.pallas import tpu as pltpu
from jax.sharding import PartitionSpec as P

MESH = pl.DeviceIdType.MESH
FIELDS = 20
BLOCKS = 64
CELLS = 512
CAP_X = 6
CAP_Z = 6
CAP_Y = 12
LIST_LEN = 48
ROWS = 24
GROUP = 8
PARTS = ((0, 2), (2, 2), (4, 2))
SENDS = ((1, 1), (1, -1), (-1, 1), (-1, -1), (0, 1), (0, -1), (1, 0), (-1, 0))
CLASS = {0: 0, -1: 1, 1: 2}
AXES = ("gx", "gy", "gz")


def kernel(
    sizes,
    fields_hbm,
    step_hbm,
    live_hbm,
    cell_hbm,
    counts_hbm,
    lists_hbm,
    out_ref,
    fields,
    step,
    live,
    cell,
    counts,
    lists,
    lists_vec,
    own,
    x_send,
    far_in,
    near_in,
    list_row,
    note_send,
    note_in,
    sum_send,
    sum_in,
    mask,
    acc,
    load_sem,
    send_sem,
    recv_sem,
    ready,
):
    def beside(**shifts):
        return {
            axis: lax.rem(lax.axis_index(axis) + shift + sizes[axis], sizes[axis])
            for axis, shift in shifts.items()
        }

    loads = [
        pltpu.make_async_copy(source, target, load_sem.at[k])
        for k, (source, target) in enumerate(
            (
                (lists_hbm, lists),
                (counts_hbm, counts),
                (lists_hbm, lists_vec),
                (step_hbm, step),
                (live_hbm, live),
                (cell_hbm, cell),
                (fields_hbm, fields),
            )
        )
    ]
    for load in loads:
        load.start()

    gx = lax.axis_index("gx")
    odd = lax.rem(gx, 2)
    toward_far = 2 * odd - 1
    early = (gx == 0) | ((odd == 1) & (gx != sizes["gx"] - 1))
    barrier = pltpu.get_barrier_semaphore()

    def greet(where):
        pl.semaphore_signal(barrier, inc=1, device_id=where, device_id_type=MESH)

    greet(beside(gx=-toward_far))
    for dz, dy in SENDS:
        greet(beside(gz=dz, gy=dy))

    @pl.when(early)
    def _():
        greet(beside(gx=toward_far))

    far_slot, near_slot = CAP_X * odd, CAP_X * (1 - odd)
    far_id, near_id = BLOCKS + far_slot, BLOCKS + near_slot

    for load in loads:
        load.wait()

    row = lax.broadcasted_iota(jnp.int32, (8, 128), 0)

    def prepare(block, _):
        columns = pl.ds(pl.multiple_of(block * 128, 128), 128)
        one = pl.ds(block, 1)
        weight = jnp.broadcast_to(live[one, :].astype(jnp.float32), (8, 128))
        length = jnp.broadcast_to(step[one, :], (8, 128))
        place = jnp.broadcast_to(cell[one, :].astype(jnp.float32), (8, 128))
        first = fields[0:8, columns]
        moved = first + length * pltpu.roll(first, 5, 0)
        first = jnp.where(row < 3, moved, first)
        tail = jnp.where(row[0:4] == 0, place[0:4], 0.0)
        last = jnp.concatenate([fields[16:20, columns] * weight[0:4], tail], axis=0)
        own[block, 0:8, :] = first * weight
        own[block, 8:16, :] = fields[8:16, columns] * weight
        own[block, 16:24, :] = last
        return 0

    lax.fori_loop(0, BLOCKS, prepare, 0, unroll=8)

    for slot in range(2 * CAP_X):
        valid = slot % CAP_X < counts[0, slot // CAP_X]
        entry = jnp.clip(lists[0, slot], 0, BLOCKS - 1)
        x_send[slot] = jnp.where(valid, own[entry], 0.0)

    def describe(at, source, target, where):
        return pltpu.make_async_remote_copy(
            src_ref=source,
            dst_ref=target,
            send_sem=send_sem.at[at],
            recv_sem=recv_sem.at[at],
            device_id=where,
            device_id_type=MESH,
        )

    def remote(*what):
        copy = describe(*what)
        copy.start()
        return copy

    pl.semaphore_wait(barrier, jnp.where(early, len(SENDS) + 1, len(SENDS) + 2))
    far_copies = []
    for k, (at, size) in enumerate(PARTS):
        source = x_send.at[pl.ds(far_slot + at, size)]
        target = far_in.at[pl.ds(at, size)]
        far_copies.append(describe(k, source, target, beside(gx=toward_far)))

    @pl.when(jnp.logical_not(early))
    def _():
        pl.semaphore_signal(
            ready, inc=1, device_id=beside(gx=toward_far), device_id_type=MESH
        )
        for copy in far_copies:
            copy.start()

    at = len(PARTS)
    near_copy = remote(
        at, x_send.at[pl.ds(near_slot, CAP_X)], near_in, beside(gx=-toward_far)
    )

    lane = lax.broadcasted_iota(jnp.int32, (1, LIST_LEN), 1)
    limit = jnp.zeros((1, LIST_LEN), jnp.int32)
    begin = 0
    for column, extent in enumerate((CAP_X, CAP_X, CAP_Z, CAP_Z, CAP_Y, CAP_Y)):
        inside = (lane >= begin) & (lane < begin + extent)
        limit = jnp.where(inside, counts[0, column] + begin, limit)
        begin += extent
    named = jnp.where(lane < limit, lists_vec[...], -1).astype(jnp.float32)
    list_row[...] = jnp.full_like(list_row, -1.0)
    list_row[:, 0:LIST_LEN] = jnp.broadcast_to(named, (8, LIST_LEN))
    named = list_row[0:1, :]
    spot = lax.broadcasted_iota(jnp.int32, (1, 128), 1)
    first_z, first_y = 2 * CAP_X, 2 * CAP_X + 2 * CAP_Z
    offset = spot - first_z
    kept = BLOCKS + 2 * CAP_X + jnp.where(offset < CAP_Z, offset + CAP_Z, offset - CAP_Z)
    at_row = lax.broadcasted_iota(jnp.int32, (LIST_LEN, 128), 0)
    at_lane = lax.broadcasted_iota(jnp.int32, (LIST_LEN, 128), 1)
    tall = jnp.broadcast_to(named, (LIST_LEN, 128))
    tall = jnp.sum(jnp.where(at_row == at_lane, tall, 0.0), axis=1, keepdims=True)
    same = jnp.where(tall == kept.astype(jnp.float32), 1.0, 0.0)
    down = jnp.max(same[first_y : first_y + CAP_Y], axis=0, keepdims=True)
    up = jnp.max(same[first_y + CAP_Y :], axis=0, keepdims=True)
    note_send[...] = jnp.where(row == 0, 1.0 - down - up, jnp.where(row == 1, down, up))
    note_copies = [
        remote(at + 1, note_send, note_in.at[0], beside(gz=1)),
        remote(at + 2, note_send, note_in.at[1], beside(gz=-1)),
    ]
    at += 3

    total = mask.shape[1]
    block_id = lax.broadcasted_iota(jnp.int32, (total, 128), 0).astype(jnp.float32)
    hit = jnp.where(block_id == named, 1.0, 0.0)

    def between(start, extent):
        return jnp.where((spot >= start) & (spot < start + extent), 1.0, 0.0)

    def select(c, lanes):
        found = jnp.max(hit * lanes, axis=1, keepdims=True)
        if c == 0:
            found = 1.0 - found
        mask[c] = jnp.broadcast_to(found, (total, 128))

    select(0, jnp.ones((1, 128), jnp.float32))
    select(1, between(first_y, CAP_Y))
    select(2, between(first_y + CAP_Y, CAP_Y))
    acc[...] = jnp.zeros_like(acc)
    for copy in note_copies:
        copy.wait_recv()
    for side in range(2):
        part = between(first_z + CAP_Z * side, CAP_Z)
        for kind in range(3):
            select(3 + 3 * side + kind, note_in[side, kind : kind + 1, :] * part)

    tile = lax.broadcasted_iota(jnp.int32, (CELLS, 128), 0).astype(jnp.float32)

    def binned(source, start, first_id, count):
        hot, values = [], [[] for _ in range(9)]
        for k in range(count):
            block = source[start + k]
            hot.append(jnp.where(tile == block[20:21, :], 1.0, 0.0).astype(jnp.bfloat16))
            high = block.astype(jnp.bfloat16).astype(jnp.float32)
            both = jnp.concatenate([high, block - high], axis=0)
            for c in range(9):
                weight = mask[c, pl.ds(first_id + k, 1), :]
                values[c].append((both * weight).astype(jnp.bfloat16))
        left = jnp.concatenate([jnp.concatenate(v, axis=1) for v in values], axis=0)
        right = jnp.concatenate(hot, axis=1)
        return lax.dot_general(
            left, right, (((1,), (1,)), ((), ())), preferred_element_type=jnp.float32
        )

    def own_group(group, _):
        start = group * GROUP
        acc[...] += binned(own, start, start, GROUP)
        return 0

    lax.fori_loop(0, BLOCKS // GROUP, own_group, 0)
    near_copy.wait_recv()
    acc[...] += binned(near_in, 0, near_id, CAP_X)

    @pl.when(early)
    def _():
        pl.semaphore_wait(ready, 1)
        for copy in far_copies:
            copy.start()

    for (start, size), copy in zip(PARTS, far_copies, strict=True):
        copy.wait_recv()
        acc[...] += binned(far_in, start, far_id + start, size)

    def packed(dz, dy):
        first = 144 * CLASS[dz] + 48 * CLASS[dy]
        sums = acc[first : first + 24] + acc[first + 24 : first + 48]
        tiles = [sums[8 * r : 8 * r + 8, 128 * k : 128 * k + 128] for r in (0, 1) for k in range(4)]
        for k in (0, 256):
            pair = [sums[16:20, k : k + 128], sums[16:20, k + 128 : k + 256]]
            tiles.append(jnp.concatenate(pair, axis=0))
        return tiles

    sum_copies = []
    for m, (dz, dy) in enumerate(SENDS):
        for k, part in enumerate(packed(dz, dy)):
            sum_send[m, k] = part
        sum_copies.append(
            remote(at + m, sum_send.at[m], sum_in.at[m], beside(gz=dz, gy=dy))
        )
    result = packed(0, 0)
    for m, copy in enumerate(sum_copies):
        copy.wait_recv()
        result = [part + sum_in[m, k] for k, part in enumerate(result)]
    for k in range(4):
        columns = slice(128 * k, 128 * k + 128)
        out_ref[0:8, columns] = result[k]
        out_ref[8:16, columns] = result[4 + k]
        half = 4 * (k % 2)
        out_ref[16:20, columns] = result[8 + k // 2][half : half + 4]
    for copy in far_copies + [near_copy] + note_copies + sum_copies:
        copy.wait_send()


def solution(mesh):
    sizes = dict(mesh.shape)

    def per_device(particle_fields, step_length, live_mask, dest_cell, block_counts, block_lists):
        anywhere = pl.BlockSpec(memory_space=pl.ANY)
        copies = len(PARTS) + 3 + len(SENDS)
        return pl.pallas_call(
            functools.partial(kernel, sizes),
            out_shape=pltpu.VMEM((FIELDS, CELLS), jnp.float32),
            in_specs=[anywhere] * 6,
            out_specs=pl.BlockSpec(memory_space=pltpu.VMEM),
            scratch_shapes=[
                pltpu.VMEM((FIELDS, BLOCKS * 128), jnp.float32),
                pltpu.VMEM((BLOCKS, 128), jnp.float32),
                pltpu.VMEM((BLOCKS, 128), jnp.int32),
                pltpu.VMEM((BLOCKS, 128), jnp.int32),
                pltpu.SMEM((1, 6), jnp.int32),
                pltpu.SMEM((1, LIST_LEN), jnp.int32),
                pltpu.VMEM((1, LIST_LEN), jnp.int32),
                pltpu.VMEM((BLOCKS, ROWS, 128), jnp.float32),
                pltpu.VMEM((2 * CAP_X, ROWS, 128), jnp.float32),
                pltpu.VMEM((CAP_X, ROWS, 128), jnp.float32),
                pltpu.VMEM((CAP_X, ROWS, 128), jnp.float32),
                pltpu.VMEM((8, 128), jnp.float32),
                pltpu.VMEM((8, 128), jnp.float32),
                pltpu.VMEM((2, 8, 128), jnp.float32),
                pltpu.VMEM((len(SENDS), 10, 8, 128), jnp.float32),
                pltpu.VMEM((len(SENDS), 10, 8, 128), jnp.float32),
                pltpu.VMEM((9, BLOCKS + 16, 128), jnp.float32),
                pltpu.VMEM((9 * 2 * ROWS, CELLS), jnp.float32),
                pltpu.SemaphoreType.DMA((7,)),
                pltpu.SemaphoreType.DMA((copies,)),
                pltpu.SemaphoreType.DMA((copies,)),
                pltpu.SemaphoreType.REGULAR,
            ],
            compiler_params=pltpu.CompilerParams(collective_id=0, has_side_effects=True),
        )(
            particle_fields,
            step_length.reshape(BLOCKS, 128),
            live_mask.reshape(BLOCKS, 128),
            dest_cell.reshape(BLOCKS, 128),
            block_counts,
            block_lists,
        )

    placed = (P(None, AXES), P(AXES), P(AXES), P(AXES), P(AXES, None), P(AXES, None))
    return jax.shard_map(
        per_device, mesh=mesh, in_specs=placed, out_specs=P(None, AXES), check_vma=False
    )
```

time: 36.1 us -> 34.1 us (0.945)
  the two profiles are of different devices: /device:TPU:24 before, /device:TPU:16 now
where the time goes in v4:
time: 34.1 us; the launch traced here: 33.9 us
  Pallas kernels  33.3 us (98%)
  local copies, waits for them, and re-layouts  0.62 us (2%)
    pallas_call x1, Pallas kernels, per_device(): pl.pallas_call(functools.partial(kernel, sizes), out_shape=pltpu.VMEM((FI...  33.3 us

profile of v4, /device:TPU:16, one launch (start us, length us, event | category | flops | bytes accessed | tf_op | source)
XLA Modules:
  0.0 33.9 jit_solution(776206720703327283)
XLA Ops:
  0.0 33.3 %shard_map.64 = f32[20,512]{1,0:T(8,128)S(1)} custom-call(f32[20,8192]{1,0:T(8,128)} %fields_hbm.1, f32[64,128]{1,0:T(8,128)} %bitcast.3, s32[64,128]{1,0:T(8,128)} %bitcast.4, s32[64,128]{1,0:T(8,128)} %bitcast.5, s32[1,6]{1,0:T(1,128)} %counts_hbm.1, s32[1,48]{1,0:T(1,128)} %lists_hbm.1), custom_call_target="tpu_custom_call" | custom-call | tf_op jit(solution)/shard_map/pallas_call | solution.py:290
  33.3 0.6 %copy.8 = f32[20,512]{1,0:T(8,128)} copy(f32[20,512]{1,0:T(8,128)S(1)} %shard_map.64) | data formatting | bytes 81920

commit v5 on v4

--- a/solution.py
+++ b/solution.py
@@ -17,7 +17,7 @@
 LIST_LEN = 48
 ROWS = 24
 GROUP = 8
-PARTS = ((0, 2), (2, 2), (4, 2))
+PARTS = ((0, 6), (6, 5), (11, 5))
 SENDS = ((1, 1), (1, -1), (-1, 1), (-1, -1), (0, 1), (0, -1), (1, 0), (-1, 0))
 CLASS = {0: 0, -1: 1, 1: 2}
 AXES = ("gx", "gy", "gz")
@@ -40,7 +40,8 @@
     lists,
     lists_vec,
     own,
-    x_send,
+    far_send,
+    near_send,
     far_in,
     near_in,
     list_row,
@@ -49,6 +50,8 @@
     sum_send,
     sum_in,
     mask,
+    far_mask,
+    slot_mask,
     acc,
     load_sem,
     send_sem,
@@ -121,10 +124,21 @@
 
     lax.fori_loop(0, BLOCKS, prepare, 0, unroll=8)
 
-    for slot in range(2 * CAP_X):
-        valid = slot % CAP_X < counts[0, slot // CAP_X]
-        entry = jnp.clip(lists[0, slot], 0, BLOCKS - 1)
-        x_send[slot] = jnp.where(valid, own[entry], 0.0)
+    tops, cells = [], jnp.zeros((8, 128), jnp.float32)
+    for k in range(CAP_X):
+        entry = jnp.clip(lists[0, far_slot + k], 0, BLOCKS - 1)
+        block = jnp.where(k < counts[0, odd], own[entry], 0.0)
+        tops.append(block[16:24])
+        cells = jnp.where(row == k, block[20:21], cells)
+        at = 1 + 5 * (k // 2) + 2 * (k % 2)
+        far_send[at] = block[0:8]
+        far_send[at + 1] = block[8:16]
+        if k % 2:
+            far_send[at + 2] = jnp.where(row < 4, tops[k - 1], pltpu.roll(tops[k], 4, 0))
+    far_send[0] = cells
+    for k in range(CAP_X):
+        entry = jnp.clip(lists[0, near_slot + k], 0, BLOCKS - 1)
+        near_send[k] = jnp.where(k < counts[0, 1 - odd], own[entry], 0.0)
 
     def describe(at, source, target, where):
         return pltpu.make_async_remote_copy(
@@ -143,9 +157,8 @@
 
     pl.semaphore_wait(barrier, jnp.where(early, len(SENDS) + 1, len(SENDS) + 2))
     far_copies = []
-    for k, (at, size) in enumerate(PARTS):
-        source = x_send.at[pl.ds(far_slot + at, size)]
-        target = far_in.at[pl.ds(at, size)]
+    for k, part in enumerate(PARTS):
+        source, target = far_send.at[pl.ds(*part)], far_in.at[pl.ds(*part)]
         far_copies.append(describe(k, source, target, beside(gx=toward_far)))
 
     @pl.when(jnp.logical_not(early))
@@ -157,9 +170,7 @@
             copy.start()
 
     at = len(PARTS)
-    near_copy = remote(
-        at, x_send.at[pl.ds(near_slot, CAP_X)], near_in, beside(gx=-toward_far)
-    )
+    near_copy = remote(at, near_send, near_in, beside(gx=-toward_far))
 
     lane = lax.broadcasted_iota(jnp.int32, (1, LIST_LEN), 1)
     limit = jnp.zeros((1, LIST_LEN), jnp.int32)
@@ -193,38 +204,23 @@
     total = mask.shape[1]
     block_id = lax.broadcasted_iota(jnp.int32, (total, 128), 0).astype(jnp.float32)
     hit = jnp.where(block_id == named, 1.0, 0.0)
-
-    def between(start, extent):
-        return jnp.where((spot >= start) & (spot < start + extent), 1.0, 0.0)
-
-    def select(c, lanes):
-        found = jnp.max(hit * lanes, axis=1, keepdims=True)
+    above = spot >= first_y + CAP_Y
+    lists_of = (spot >= 0, (spot >= first_y) & jnp.logical_not(above), above)
+    for c, lanes in enumerate(lists_of):
+        found = jnp.max(jnp.where(lanes, hit, 0.0), axis=1, keepdims=True)
         if c == 0:
             found = 1.0 - found
         mask[c] = jnp.broadcast_to(found, (total, 128))
 
-    select(0, jnp.ones((1, 128), jnp.float32))
-    select(1, between(first_y, CAP_Y))
-    select(2, between(first_y + CAP_Y, CAP_Y))
-    acc[...] = jnp.zeros_like(acc)
-    for copy in note_copies:
-        copy.wait_recv()
-    for side in range(2):
-        part = between(first_z + CAP_Z * side, CAP_Z)
-        for kind in range(3):
-            select(3 + 3 * side + kind, note_in[side, kind : kind + 1, :] * part)
-
     tile = lax.broadcasted_iota(jnp.int32, (CELLS, 128), 0).astype(jnp.float32)
 
-    def binned(source, start, first_id, count):
-        hot, values = [], [[] for _ in range(9)]
-        for k in range(count):
-            block = source[start + k]
-            hot.append(jnp.where(tile == block[20:21, :], 1.0, 0.0).astype(jnp.bfloat16))
+    def binned(blocks):
+        hot, values = [], [[] for _ in blocks[0][2]]
+        for block, place, weights in blocks:
+            hot.append(jnp.where(tile == place, 1.0, 0.0).astype(jnp.bfloat16))
             high = block.astype(jnp.bfloat16).astype(jnp.float32)
             both = jnp.concatenate([high, block - high], axis=0)
-            for c in range(9):
-                weight = mask[c, pl.ds(first_id + k, 1), :]
+            for c, weight in enumerate(weights):
                 values[c].append((both * weight).astype(jnp.bfloat16))
         left = jnp.concatenate([jnp.concatenate(v, axis=1) for v in values], axis=0)
         right = jnp.concatenate(hot, axis=1)
@@ -232,24 +228,74 @@
             left, right, (((1,), (1,)), ((), ())), preferred_element_type=jnp.float32
         )
 
+    def weights_of(block):
+        return [mask[c, pl.ds(block, 1), :] for c in range(3)]
+
+    def whole(block, weights):
+        return block, block[20:21], weights
+
+    acc[0:144] = jnp.zeros((144, CELLS), jnp.float32)
+
     def own_group(group, _):
         start = group * GROUP
-        acc[...] += binned(own, start, start, GROUP)
+        acc[0:144] += binned(
+            [whole(own[start + k], weights_of(start + k)) for k in range(GROUP)]
+        )
         return 0
 
     lax.fori_loop(0, BLOCKS // GROUP, own_group, 0)
     near_copy.wait_recv()
-    acc[...] += binned(near_in, 0, near_id, CAP_X)
-
-    @pl.when(early)
+    acc[0:144] += binned([whole(near_in[k], weights_of(near_id + k)) for k in range(CAP_X)])
+
+    for copy in note_copies:
+        copy.wait_recv()
+    slot = lax.broadcasted_iota(jnp.int32, (16, 128), 0)
+    here = lax.broadcasted_iota(jnp.int32, (16, 128), 1) == slot + first_z
+    far_named = named == (row + far_id).astype(jnp.float32)
+    for kind in range(3):
+        kinds = [note_in[side, kind : kind + 1, :] for side in range(2)]
+        found = jnp.where(here, jnp.where(slot < CAP_Z, kinds[0], kinds[1]), 0.0)
+        found = jnp.max(found, axis=1, keepdims=True)
+        slot_mask[kind] = jnp.broadcast_to(found, (16, 128))
+        for side in range(2):
+            begin = first_z + CAP_Z * side
+            inside = (spot >= begin) & (spot < begin + CAP_Z)
+            found = jnp.where(far_named & inside, kinds[side], 0.0)
+            found = jnp.max(found, axis=1, keepdims=True)
+            far_mask[3 * side + kind] = jnp.broadcast_to(found, (8, 128))
+    for side in range(2):
+        blocks = []
+        for k in range(CAP_Z):
+            entry = lists[0, first_z + CAP_Z * side + k]
+            place = entry - near_id
+            valid = k < counts[0, 2 + side]
+            valid = valid & ((entry < BLOCKS) | ((place >= 0) & (place < CAP_X)))
+            block = own[jnp.clip(entry, 0, BLOCKS - 1)]
+            other = near_in[jnp.clip(place, 0, CAP_X - 1)]
+            block = jnp.where(valid, jnp.where(entry < BLOCKS, block, other), 0.0)
+            at_slot = CAP_Z * side + k
+            weights = [slot_mask[c, at_slot : at_slot + 1, :] for c in range(3)]
+            blocks.append(whole(block, weights))
+        acc[144 * (1 + side) : 144 * (2 + side)] = binned(blocks)
+
+    @pl.when(early & (gx != 0))
     def _():
         pl.semaphore_wait(ready, 1)
         for copy in far_copies:
             copy.start()
 
-    for (start, size), copy in zip(PARTS, far_copies, strict=True):
+    for pair, copy in enumerate(far_copies):
         copy.wait_recv()
-        acc[...] += binned(far_in, start, far_id + start, size)
+        first = 1 + 5 * pair
+        last = far_in[first + 4]
+        blocks = []
+        for k, top in ((2 * pair, last), (2 * pair + 1, pltpu.roll(last, 4, 0))):
+            start = first + 2 * (k % 2)
+            block = jnp.concatenate([far_in[start], far_in[start + 1], top], axis=0)
+            weights = weights_of(far_id + k)
+            weights += [far_mask[c, k : k + 1, :] for c in range(6)]
+            blocks.append((block, far_in[0, k : k + 1, :], weights))
+        acc[...] += binned(blocks)
 
     def packed(dz, dy):
         first = 144 * CLASS[dz] + 48 * CLASS[dy]
@@ -267,6 +313,13 @@
         sum_copies.append(
             remote(at + m, sum_send.at[m], sum_in.at[m], beside(gz=dz, gy=dy))
         )
+
+    @pl.when(gx == 0)
+    def _():
+        pl.semaphore_wait(ready, 1)
+        for copy in far_copies:
+            copy.start()
+
     result = packed(0, 0)
     for m, copy in enumerate(sum_copies):
         copy.wait_recv()
@@ -301,15 +354,18 @@
                 pltpu.SMEM((1, LIST_LEN), jnp.int32),
                 pltpu.VMEM((1, LIST_LEN), jnp.int32),
                 pltpu.VMEM((BLOCKS, ROWS, 128), jnp.float32),
-                pltpu.VMEM((2 * CAP_X, ROWS, 128), jnp.float32),
+                pltpu.VMEM((16, 8, 128), jnp.float32),
                 pltpu.VMEM((CAP_X, ROWS, 128), jnp.float32),
+                pltpu.VMEM((16, 8, 128), jnp.float32),
                 pltpu.VMEM((CAP_X, ROWS, 128), jnp.float32),
                 pltpu.VMEM((8, 128), jnp.float32),
                 pltpu.VMEM((8, 128), jnp.float32),
                 pltpu.VMEM((2, 8, 128), jnp.float32),
                 pltpu.VMEM((len(SENDS), 10, 8, 128), jnp.float32),
                 pltpu.VMEM((len(SENDS), 10, 8, 128), jnp.float32),
-                pltpu.VMEM((9, BLOCKS + 16, 128), jnp.float32),
+                pltpu.VMEM((3, BLOCKS + 16, 128), jnp.float32),
+                pltpu.VMEM((6, 8, 128), jnp.float32),
+                pltpu.VMEM((3, 16, 128), jnp.float32),
                 pltpu.VMEM((9 * 2 * ROWS, CELLS), jnp.float32),
                 pltpu.SemaphoreType.DMA((7,)),
                 pltpu.SemaphoreType.DMA((copies,)),

time: 34.1 us -> 33.7 us (0.988)
  Pallas kernels: 33.3 us -> 32.9 us
    pallas_call x1, Pallas kernels: 33.3 us -> 32.9 us  [per_device(): pl.pallas_call(functools.partial(kernel, sizes), out_shape=pltpu.VMEM((FI...]
where the time goes in v5:
time: 33.7 us; the launch traced here: 33.6 us
  Pallas kernels  32.9 us (98%)
  local copies, waits for them, and re-layouts  0.62 us (2%)
    pallas_call x1, Pallas kernels, per_device(): pl.pallas_call(functools.partial(kernel, sizes), out_shape=pltpu.VMEM((FI...  32.9 us

profile of v5, /device:TPU:16, one launch (start us, length us, event | category | flops | bytes accessed | tf_op | source)
XLA Modules:
  0.0 33.6 jit_solution(3570629910981206355)
XLA Ops:
  0.0 32.9 %shard_map.64 = f32[20,512]{1,0:T(8,128)S(1)} custom-call(f32[20,8192]{1,0:T(8,128)} %fields_hbm.1, f32[64,128]{1,0:T(8,128)} %bitcast.3, s32[64,128]{1,0:T(8,128)} %bitcast.4, s32[64,128]{1,0:T(8,128)} %bitcast.5, s32[1,6]{1,0:T(1,128)} %counts_hbm.1, s32[1,48]{1,0:T(1,128)} %lists_hbm.1), custom_call_target="tpu_custom_call" | custom-call | tf_op jit(solution)/shard_map/pallas_call | solution.py:343
  32.9 0.6 %copy.8 = f32[20,512]{1,0:T(8,128)} copy(f32[20,512]{1,0:T(8,128)S(1)} %shard_map.64) | data formatting | bytes 81920

commit v6 on v5

--- a/solution.py
+++ b/solution.py
@@ -17,8 +17,9 @@
 LIST_LEN = 48
 ROWS = 24
 GROUP = 8
+LAG = 1
 PARTS = ((0, 6), (6, 5), (11, 5))
-SENDS = ((1, 1), (1, -1), (-1, 1), (-1, -1), (0, 1), (0, -1), (1, 0), (-1, 0))
+SENDS = ((-1, 1), (1, 1), (-1, -1), (1, -1), (0, 1), (0, -1), (1, 0), (-1, 0))
 CLASS = {0: 0, -1: 1, 1: 2}
 AXES = ("gx", "gy", "gz")
 
@@ -85,6 +86,7 @@
     odd = lax.rem(gx, 2)
     toward_far = 2 * odd - 1
     early = (gx == 0) | ((odd == 1) & (gx != sizes["gx"] - 1))
+    yields = (gx == sizes["gx"] - 1) & (lax.axis_index("gy") < 3 * sizes["gy"] // 4)
     barrier = pltpu.get_barrier_semaphore()
 
     def greet(where):
@@ -166,6 +168,9 @@
         pl.semaphore_signal(
             ready, inc=1, device_id=beside(gx=toward_far), device_id_type=MESH
         )
+
+    @pl.when(jnp.logical_not(early | yields))
+    def _():
         for copy in far_copies:
             copy.start()
 
@@ -243,7 +248,14 @@
         )
         return 0
 
-    lax.fori_loop(0, BLOCKS // GROUP, own_group, 0)
+    lax.fori_loop(0, LAG, own_group, 0)
+
+    @pl.when(yields)
+    def _():
+        for copy in far_copies:
+            copy.start()
+
+    lax.fori_loop(LAG, BLOCKS // GROUP, own_group, 0)
     near_copy.wait_recv()
     acc[0:144] += binned([whole(near_in[k], weights_of(near_id + k)) for k in range(CAP_X)])
 

time: 33.7 us -> 31.9 us (0.947)
  the two profiles are of different devices: /device:TPU:16 before, /device:TPU:2 now
where the time goes in v6:
time: 31.9 us; the launch traced here: 31.8 us
  Pallas kernels  31.1 us (97%)
  local copies, waits for them, and re-layouts  0.62 us (2%)
    pallas_call x1, Pallas kernels, per_device(): pl.pallas_call(functools.partial(kernel, sizes), out_shape=pltpu.VMEM((FI...  31.1 us

profile of v6, /device:TPU:2, one launch (start us, length us, event | category | flops | bytes accessed | tf_op | source)
XLA Modules:
  0.0 31.8 jit_solution(10987628950132554724)
XLA Ops:
  0.0 31.1 %shard_map.64 = f32[20,512]{1,0:T(8,128)S(1)} custom-call(f32[20,8192]{1,0:T(8,128)} %fields_hbm.1, f32[64,128]{1,0:T(8,128)} %bitcast.3, s32[64,128]{1,0:T(8,128)} %bitcast.4, s32[64,128]{1,0:T(8,128)} %bitcast.5, s32[1,6]{1,0:T(1,128)} %counts_hbm.1, s32[1,48]{1,0:T(1,128)} %lists_hbm.1), custom_call_target="tpu_custom_call" | custom-call | tf_op jit(solution)/shard_map/pallas_call | solution.py:355
  31.2 0.6 %copy.8 = f32[20,512]{1,0:T(8,128)} copy(f32[20,512]{1,0:T(8,128)S(1)} %shard_map.64) | data formatting | bytes 81920

commit v7 on v6

--- a/solution.py
+++ b/solution.py
@@ -17,7 +17,7 @@
 LIST_LEN = 48
 ROWS = 24
 GROUP = 8
-LAG = 1
+LAG = 2
 PARTS = ((0, 6), (6, 5), (11, 5))
 SENDS = ((-1, 1), (1, 1), (-1, -1), (1, -1), (0, 1), (0, -1), (1, 0), (-1, 0))
 CLASS = {0: 0, -1: 1, 1: 2}
@@ -58,6 +58,9 @@
     send_sem,
     recv_sem,
     ready,
+    near_ok,
+    passed_on,
+    all_in,
 ):
     def beside(**shifts):
         return {
@@ -86,19 +89,29 @@
     odd = lax.rem(gx, 2)
     toward_far = 2 * odd - 1
     early = (gx == 0) | ((odd == 1) & (gx != sizes["gx"] - 1))
-    yields = (gx == sizes["gx"] - 1) & (lax.axis_index("gy") < 3 * sizes["gy"] // 4)
     barrier = pltpu.get_barrier_semaphore()
 
     def greet(where):
         pl.semaphore_signal(barrier, inc=1, device_id=where, device_id_type=MESH)
 
-    greet(beside(gx=-toward_far))
-    for dz, dy in SENDS:
-        greet(beside(gz=dz, gy=dy))
+    last_row = gx == sizes["gx"] - 1
+    by_last = gx == sizes["gx"] - 2
+
+    @pl.when(jnp.logical_not(by_last))
+    def _():
+        greet(beside(gx=-toward_far))
+
+    @pl.when(jnp.logical_not(last_row))
+    def _():
+        for dz, dy in SENDS:
+            greet(beside(gz=dz, gy=dy))
+
 
     @pl.when(early)
     def _():
         greet(beside(gx=toward_far))
+
+    yields = last_row & (lax.axis_index("gy") < 3 * sizes["gy"] // 4)
 
     far_slot, near_slot = CAP_X * odd, CAP_X * (1 - odd)
     far_id, near_id = BLOCKS + far_slot, BLOCKS + near_slot
@@ -157,7 +170,8 @@
         copy.start()
         return copy
 
-    pl.semaphore_wait(barrier, jnp.where(early, len(SENDS) + 1, len(SENDS) + 2))
+    greeted = jnp.where(early, len(SENDS) + 1, len(SENDS) + 2)
+    pl.semaphore_wait(barrier, jnp.where(last_row, 1, greeted))
     far_copies = []
     for k, part in enumerate(PARTS):
         source, target = far_send.at[pl.ds(*part)], far_in.at[pl.ds(*part)]
@@ -175,7 +189,18 @@
             copy.start()
 
     at = len(PARTS)
-    near_copy = remote(at, near_send, near_in, beside(gx=-toward_far))
+    near_copy = describe(at, near_send, near_in, beside(gx=-toward_far))
+
+    @pl.when(jnp.logical_not(last_row))
+    def _():
+        near_copy.start()
+
+    @pl.when(by_last)
+    def _():
+        pl.semaphore_signal(
+            near_ok, inc=1, device_id=beside(gx=-toward_far), device_id_type=MESH
+        )
+
 
     lane = lax.broadcasted_iota(jnp.int32, (1, LIST_LEN), 1)
     limit = jnp.zeros((1, LIST_LEN), jnp.int32)
@@ -201,9 +226,15 @@
     up = jnp.max(same[first_y + CAP_Y :], axis=0, keepdims=True)
     note_send[...] = jnp.where(row == 0, 1.0 - down - up, jnp.where(row == 1, down, up))
     note_copies = [
-        remote(at + 1, note_send, note_in.at[0], beside(gz=1)),
-        remote(at + 2, note_send, note_in.at[1], beside(gz=-1)),
+        describe(at + 1, note_send, note_in.at[0], beside(gz=1)),
+        describe(at + 2, note_send, note_in.at[1], beside(gz=-1)),
     ]
+
+    @pl.when(jnp.logical_not(last_row))
+    def _():
+        for copy in note_copies:
+            copy.start()
+
     at += 3
 
     total = mask.shape[1]
@@ -256,8 +287,20 @@
             copy.start()
 
     lax.fori_loop(LAG, BLOCKS // GROUP, own_group, 0)
+
+    @pl.when(last_row)
+    def _():
+        pl.semaphore_wait(near_ok, 1)
+        near_copy.start()
+
     near_copy.wait_recv()
     acc[0:144] += binned([whole(near_in[k], weights_of(near_id + k)) for k in range(CAP_X)])
+
+    @pl.when(last_row)
+    def _():
+        pl.semaphore_wait(all_in, 1)
+        for copy in note_copies:
+            copy.start()
 
     for copy in note_copies:
         copy.wait_recv()
@@ -290,6 +333,14 @@
             blocks.append(whole(block, weights))
         acc[144 * (1 + side) : 144 * (2 + side)] = binned(blocks)
 
+    @pl.when(gx == 0)
+    def _():
+        pl.semaphore_wait(ready, 1)
+        for dz, dy in SENDS:
+            pl.semaphore_signal(
+                passed_on, inc=1, device_id=beside(gz=dz, gy=dy), device_id_type=MESH
+            )
+
     @pl.when(early & (gx != 0))
     def _():
         pl.semaphore_wait(ready, 1)
@@ -328,9 +379,12 @@
 
     @pl.when(gx == 0)
     def _():
-        pl.semaphore_wait(ready, 1)
         for copy in far_copies:
             copy.start()
+        pl.semaphore_wait(passed_on, len(SENDS))
+        pl.semaphore_signal(
+            all_in, inc=1, device_id=beside(gx=toward_far), device_id_type=MESH
+        )
 
     result = packed(0, 0)
     for m, copy in enumerate(sum_copies):
@@ -383,6 +437,9 @@
                 pltpu.SemaphoreType.DMA((copies,)),
                 pltpu.SemaphoreType.DMA((copies,)),
                 pltpu.SemaphoreType.REGULAR,
+                pltpu.SemaphoreType.REGULAR,
+                pltpu.SemaphoreType.REGULAR,
+                pltpu.SemaphoreType.REGULAR,
             ],
             compiler_params=pltpu.CompilerParams(collective_id=0, has_side_effects=True),
         )(

time: 31.9 us -> 31.1 us (0.975)
  the two profiles are of different devices: /device:TPU:2 before, /device:TPU:24 now
where the time goes in v7:
time: 31.1 us; the launch traced here: 30.9 us
  Pallas kernels  30.3 us (97%)
  local copies, waits for them, and re-layouts  0.62 us (2%)
    pallas_call x1, Pallas kernels, per_device(): pl.pallas_call(functools.partial(kernel, sizes), out_shape=pltpu.VMEM((FI...  30.3 us
    unnamed x1, local copies, waits for them, and re-layouts  0.62 us

profile of v7, /device:TPU:24, one launch (start us, length us, event | category | flops | bytes accessed | tf_op | source)
XLA Modules:
  0.0 30.9 jit_solution(15291043451364705370)
XLA Ops:
  0.0 30.3 %shard_map.64 = f32[20,512]{1,0:T(8,128)S(1)} custom-call(f32[20,8192]{1,0:T(8,128)} %fields_hbm.1, f32[64,128]{1,0:T(8,128)} %bitcast.3, s32[64,128]{1,0:T(8,128)} %bitcast.4, s32[64,128]{1,0:T(8,128)} %bitcast.5, s32[1,6]{1,0:T(1,128)} %counts_hbm.1, s32[1,48]{1,0:T(1,128)} %lists_hbm.1), custom_call_target="tpu_custom_call" | custom-call | tf_op jit(solution)/shard_map/pallas_call | solution.py:409
  30.3 0.6 %copy.8 = f32[20,512]{1,0:T(8,128)} copy(f32[20,512]{1,0:T(8,128)S(1)} %shard_map.64) | data formatting | bytes 81920

commit v8 on v7

--- a/solution.py
+++ b/solution.py
@@ -68,17 +68,18 @@
             for axis, shift in shifts.items()
         }
 
+    quarters = [pl.ds(16 * 128 * k, 16 * 128) for k in range(4)]
     loads = [
         pltpu.make_async_copy(source, target, load_sem.at[k])
         for k, (source, target) in enumerate(
             (
+                *((fields_hbm.at[:, q], fields.at[:, q]) for q in quarters),
                 (lists_hbm, lists),
                 (counts_hbm, counts),
                 (lists_hbm, lists_vec),
                 (step_hbm, step),
                 (live_hbm, live),
                 (cell_hbm, cell),
-                (fields_hbm, fields),
             )
         )
     ]
@@ -137,7 +138,7 @@
         own[block, 16:24, :] = last
         return 0
 
-    lax.fori_loop(0, BLOCKS, prepare, 0, unroll=8)
+    lax.fori_loop(0, BLOCKS, prepare, 0, unroll=16)
 
     tops, cells = [], jnp.zeros((8, 128), jnp.float32)
     for k in range(CAP_X):
@@ -151,10 +152,6 @@
         if k % 2:
             far_send[at + 2] = jnp.where(row < 4, tops[k - 1], pltpu.roll(tops[k], 4, 0))
     far_send[0] = cells
-    for k in range(CAP_X):
-        entry = jnp.clip(lists[0, near_slot + k], 0, BLOCKS - 1)
-        near_send[k] = jnp.where(k < counts[0, 1 - odd], own[entry], 0.0)
-
     def describe(at, source, target, where):
         return pltpu.make_async_remote_copy(
             src_ref=source,
@@ -189,6 +186,10 @@
             copy.start()
 
     at = len(PARTS)
+    for k in range(CAP_X):
+        entry = jnp.clip(lists[0, near_slot + k], 0, BLOCKS - 1)
+        near_send[k] = jnp.where(k < counts[0, 1 - odd], own[entry], 0.0)
+
     near_copy = describe(at, near_send, near_in, beside(gx=-toward_far))
 
     @pl.when(jnp.logical_not(last_row))
@@ -433,7 +434,7 @@
                 pltpu.VMEM((6, 8, 128), jnp.float32),
                 pltpu.VMEM((3, 16, 128), jnp.float32),
                 pltpu.VMEM((9 * 2 * ROWS, CELLS), jnp.float32),
-                pltpu.SemaphoreType.DMA((7,)),
+                pltpu.SemaphoreType.DMA((10,)),
                 pltpu.SemaphoreType.DMA((copies,)),
                 pltpu.SemaphoreType.DMA((copies,)),
                 pltpu.SemaphoreType.REGULAR,

time: 31.1 us -> 31.1 us (level)
  no operation moved by 1% of the time
where the time goes in v8:
time: 31.1 us; the launch traced here: 30.9 us
  Pallas kernels  30.3 us (97%)
  local copies, waits for them, and re-layouts  0.62 us (2%)
    pallas_call x1, Pallas kernels, per_device(): pl.pallas_call(functools.partial(kernel, sizes), out_shape=pltpu.VMEM((FI...  30.3 us
    unnamed x1, local copies, waits for them, and re-layouts  0.62 us

profile of v8, /device:TPU:24, one launch (start us, length us, event | category | flops | bytes accessed | tf_op | source)
XLA Modules:
  0.0 30.9 jit_solution(14691582882496984039)
XLA Ops:
  0.0 30.3 %shard_map.64 = f32[20,512]{1,0:T(8,128)S(1)} custom-call(f32[20,8192]{1,0:T(8,128)} %fields_hbm.1, f32[64,128]{1,0:T(8,128)} %bitcast.3, s32[64,128]{1,0:T(8,128)} %bitcast.4, s32[64,128]{1,0:T(8,128)} %bitcast.5, s32[1,6]{1,0:T(1,128)} %counts_hbm.1, s32[1,48]{1,0:T(1,128)} %lists_hbm.1), custom_call_target="tpu_custom_call" | custom-call | tf_op jit(solution)/shard_map/pallas_call | solution.py:410
  30.3 0.6 %copy.8 = f32[20,512]{1,0:T(8,128)} copy(f32[20,512]{1,0:T(8,128)S(1)} %shard_map.64) | data formatting | bytes 81920
